TPU v7x, 32 devices: a whole 2x2x4 slice. The times are simulated.
32 devices in a mesh: blk: 8 (over y, x, core), inner: 4 (over z).
Axes of the slice: x: 2, y: 2, z: 4, core: 2. Of those that a mesh axis runs over, the one named last changes fastest.
Arguments:
- query_latent: bfloat16 [1024, 16384], P('blk', 'inner'), may hold values from -100 to 100
- query_rotary: bfloat16 [1024, 2048], P('blk', 'inner'), may hold values from -100 to 100
- upstream: bfloat16 [1024, 16384], P('blk', 'inner'), may hold values from -6 to 6
- latent: bfloat16 [1024, 512], P(('blk', 'inner')), may hold values from -8 to 8
- key_rotary: bfloat16 [1024, 64], P(('blk', 'inner')), may hold values from -8 to 8
- pattern: int32 [8, 5], P('blk'), may hold values from -1 to 7, as said below
Outputs:
- query_cotangent: bfloat16 [1024, 16384], P('blk', 'inner')
- rotary_cotangent: bfloat16 [1024, 2048], P('blk', 'inner')
- latent_cotangent: float32 [1024, 512], P(('blk', 'inner'))
- positional_cotangent: float32 [1024, 64], P(('blk', 'inner'))
Inputs may be any that keep to these rules, and one draw needn't show every extreme that they name: `pattern`: let d_0 < d_1 < ... be the distinct numbers among 0 to 1 and m * 1 for m = 1 to 4; there are 5 of them. Entry k of row q is either q - d_k or -1, and it is -1 whenever q - d_k < 0. Entry 0 of every row is q.
All inputs are finite; a program needn't handle non-finite values.
Results may differ from a plain program's by a relative error of at most 0.0085.
Values may be sent and summed in bfloat16 or wider, within the bound.
No kernel may reach another device: no remote copies, remote signals or barrier semaphores. Data moves between devices by JAX's collectives and lax.ppermute only.
A program may use at most 128 MiB of HBM per device.

v0:
```python
import functools

import jax
import jax.numpy as jnp
from jax import lax
from jax.experimental import pallas as pl
from jax.experimental.pallas import tpu as pltpu
from jax.sharding import PartitionSpec as P


NOPE = 128
WIN = 2
NSTR = 4
LOG2E = 1.4426950408889634
FLOOR = -1e30
BF16 = jnp.bfloat16
F32 = jnp.float32
VMEM = 24 * 1024 * 1024


def spacing_list(blocks):
    spacing = blocks // 8
    listed = set(range(WIN))
    for number in range(1, NSTR + 1):
        listed.add(number * spacing)
    return sorted(listed)


def rotated(value, axis, steps):
    count = lax.axis_size(axis)
    return lax.ppermute(value, axis, [(s, (s + steps) % count) for s in range(count)])


def swapped(value):
    count = lax.axis_size("blk")
    return lax.ppermute(value, "blk", [(s, s + 1 - 2 * (s % 2)) for s in range(count)])


def stacked_rope(rope_pair, rope):
    lane = lax.broadcasted_iota(jnp.int32, rope_pair.shape, 1)
    zero = jnp.zeros_like(rope_pair)
    return jnp.concatenate(
        [jnp.where(lane < rope, rope_pair, zero), jnp.where(lane >= rope, rope_pair, zero)], axis=0
    )


def stage_kernel(dims, x_ref, *refs):
    heads, tokens, latent, rope = dims
    *rope_refs, out_ref, sems = refs
    copies = []
    for h in range(heads):
        rows = slice(h * tokens, (h + 1) * tokens)
        cols = slice(h * latent, (h + 1) * latent)
        copies.append(
            pltpu.make_async_copy(x_ref.at[:, cols], out_ref.at[rows, :latent], sems.at[h])
        )
    for copy in copies:
        copy.start()
    for ref in rope_refs:
        for p in range(heads // 2):
            rows = slice(2 * p * tokens, 2 * (p + 1) * tokens)
            out_ref[rows, latent:] = stacked_rope(ref[:, 2 * p * rope : 2 * (p + 1) * rope], rope)
    for copy in copies:
        copy.wait()


def merge_kernel(late_ref, met_ref, four_ref, two_ref):
    tokens = two_ref.shape[0]
    odd = lax.rem(lax.axis_index("blk"), 2) == 1
    one, three = met_ref[:tokens].astype(F32), met_ref[tokens:].astype(F32)
    four_ref[...] = (late_ref[:tokens] + jnp.where(odd, three, 0.0)).astype(BF16)
    two_ref[...] = (late_ref[tokens:] + jnp.where(odd, one, three)).astype(BF16)


def total_kernel(returned, own_ref, *refs):
    total = own_ref[...]
    for ref in refs[:returned]:
        total += ref[...].astype(F32)
    for k, ref in enumerate(refs[returned:]):
        shard = ref.shape[0]
        ref[...] = total[k * shard : (k + 1) * shard].astype(ref.dtype)


def finish_kernel(dims, own_ref, *refs):
    latent, rope = dims
    *parts, latent_ref, rope_ref = refs
    total = own_ref[...]
    for part in parts:
        total += part[...].astype(F32)
    latent_ref[...] = total[:, :latent]
    rope_ref[...] = total[:, latent : latent + rope] + total[:, latent + rope :]


def key_gradient(ds, weights, q2, u2, latent):
    nn = (((1,), (0,)), ((), ()))
    part = lax.dot_general(ds, q2, nn, preferred_element_type=F32)
    mixed = lax.dot_general(weights, u2, nn, preferred_element_type=F32)
    return part[:, :latent] + mixed, part[:, latent:]


def place_keys(keys, key_refs, sources, tokens):
    odd = lax.rem(lax.axis_index("blk"), 2) == 1
    for d, source in enumerate(sources):
        block = key_refs[source[0]][...]
        if len(source) == 2:
            block = jnp.where(odd, key_refs[source[1]][...], block)
        keys[d * tokens : (d + 1) * tokens, :] = block


def products(keys, q2_ref, u2_ref, lanes, latent):
    nt = (((1,), (1,)), ((), ()))
    s = lax.dot_general(keys[...], q2_ref[lanes, :], nt, preferred_element_type=F32)
    p = lax.dot_general(keys[:, :latent], u2_ref[lanes, :], nt, preferred_element_type=F32)
    return s, p


def early_kernel(dims, sources, entries, pattern_ref, q2_ref, u2_ref, *refs):
    pairs, tokens, shard, latent, scale = dims
    e_ref, p_ref, stats_ref, keys = refs[-4:]
    place_keys(keys, refs[:-4], sources, tokens)
    row = lax.broadcasted_iota(jnp.int32, (tokens, 2 * tokens), 0)
    col = lax.broadcasted_iota(jnp.int32, (tokens, 2 * tokens), 1)
    slots = tokens // shard
    owner = lax.rem(lax.axis_index("inner") - row // shard + slots, slots)
    causal = owner * shard + lax.rem(row, shard) <= lax.rem(col, tokens)
    span = lambda p: slice(2 * p * tokens, 2 * (p + 1) * tokens)

    def fill(p):
        lanes = span(p)
        e_ref[:, lanes], p_ref[:, lanes] = products(keys, q2_ref, u2_ref, lanes, latent)

    fill(0)
    for p in range(pairs):
        if p + 1 < pairs:
            fill(p + 1)
        lanes = span(p)
        peak = None
        for d, entry in enumerate(entries):
            rows = slice(d * tokens, (d + 1) * tokens)
            allowed = pattern_ref[0, entry] >= 0
            if entry == 0:
                allowed = jnp.logical_and(causal, allowed)
            s = jnp.where(allowed, e_ref[rows, lanes] * (scale * LOG2E), -jnp.inf)
            e_ref[rows, lanes] = s
            top = jnp.max(s, axis=0, keepdims=True)
            peak = top if peak is None else jnp.maximum(peak, top)
        peak = jnp.maximum(peak, FLOOR)
        total = jnp.zeros_like(peak)
        mixed = jnp.zeros_like(peak)
        for d in range(len(entries)):
            rows = slice(d * tokens, (d + 1) * tokens)
            e = jnp.exp2(e_ref[rows, lanes] - peak)
            e_ref[rows, lanes] = e
            total += jnp.sum(e, axis=0, keepdims=True)
            mixed += jnp.sum(e * p_ref[rows, lanes], axis=0, keepdims=True)
        stats_ref[0:1, lanes] = peak
        stats_ref[1:2, lanes] = total
        stats_ref[2:3, lanes] = mixed


def scores_kernel(dims, groups, sources, entries, pattern_ref, q2_ref, u2_ref, *refs):
    nd, kept, pairs, tokens, latent, scale = dims
    early = [refs[3 * g : 3 * g + 3] for g in range(len(groups))]
    ds_ref, kept_ref, keys, grad_ref, tail, s_scr, t_scr, w_scr = refs[-8:]
    key_refs = refs[3 * len(groups) : -8]
    place_keys(keys, key_refs, sources, tokens)
    later = [d for d in range(nd) if not any(d in group for group in groups)]
    place_keys(tail, key_refs, [sources[d] for d in later], tokens)
    chosen = [pattern_ref[0, entries[d]] >= 0 for d in later]
    span = lambda p: slice(2 * p * tokens, 2 * (p + 1) * tokens)
    block = lambda k: slice(k * tokens, (k + 1) * tokens)

    def fill(p):
        s_scr[p % 2], t_scr[p % 2] = products(tail, q2_ref, u2_ref, span(p), latent)

    fill(0)
    for p in range(pairs):
        if p + 1 < pairs:
            fill(p + 1)
        lanes = span(p)
        slot = p % 2
        before = [stats_ref[0:1, lanes] for _, _, stats_ref in early]
        peak = functools.reduce(jnp.maximum, before)
        for k in range(len(later)):
            s = jnp.where(chosen[k], s_scr[slot, block(k), :] * (scale * LOG2E), -jnp.inf)
            s_scr[slot, block(k), :] = s
            peak = jnp.maximum(peak, jnp.max(s, axis=0, keepdims=True))
        shrink = [jnp.exp2(b - peak) for b in before]
        total = sum(f * refs3[2][1:2, lanes] for f, refs3 in zip(shrink, early))
        mixed = sum(f * refs3[2][2:3, lanes] for f, refs3 in zip(shrink, early))
        for k in range(len(later)):
            e = jnp.exp2(s_scr[slot, block(k), :] - peak)
            s_scr[slot, block(k), :] = e
            total += jnp.sum(e, axis=0, keepdims=True)
            mixed += jnp.sum(e * t_scr[slot, block(k), :], axis=0, keepdims=True)
        inverse = 1.0 / total
        correction = mixed * inverse
        factors = [f * inverse for f in shrink]
        for d in range(nd):
            if d in later:
                k = later.index(d)
                e, dp, factor = s_scr[slot, block(k), :], t_scr[slot, block(k), :], inverse
            else:
                g = [d in group for group in groups].index(True)
                source = block(groups[g].index(d))
                e, dp, factor = early[g][0][source, lanes], early[g][1][source, lanes], factors[g]
            w = (e * factor).astype(BF16)
            if d < kept:
                kept_ref[block(d), lanes] = w
            else:
                w_scr[block(d - kept), lanes] = w
            ds_ref[block(d), lanes] = (e * (factor * scale) * (dp - correction)).astype(BF16)
    main, turned = key_gradient(
        ds_ref[kept * tokens :, :], w_scr[...], q2_ref[...], u2_ref[...], latent
    )
    grad_ref[:, :latent] = main.astype(BF16)
    grad_ref[:, latent:] = turned.astype(BF16)


def gradient_kernel(dims, ds_ref, w_ref, q2_ref, u2_ref, grad_ref):
    late, latent = dims
    main, turned = key_gradient(
        ds_ref[:late, :], w_ref[:late, :], q2_ref[...], u2_ref[...], latent
    )
    grad_ref[:, :latent] = main
    grad_ref[:, latent:] = turned


def own_kernel(dims, ds_ref, w_ref, q2_ref, u2_ref, keys_ref, *refs):
    own, pairs, tokens, latent, rope = dims
    *met_refs, grad_ref, dq_ref, dr_ref, dq_scr, dr_scr, sems = refs
    tn = (((0,), (0,)), ((), ()))
    lane = lax.broadcasted_iota(jnp.int32, (tokens, 2 * rope), 1)
    copies = []
    for p in range(pairs):
        lanes = slice(2 * p * tokens, 2 * (p + 1) * tokens)
        dq = lax.dot_general(ds_ref[:, lanes], keys_ref[...], tn, preferred_element_type=F32)
        even, odd = dq[:tokens], dq[tokens:]
        out = 2 * p * latent
        dq_scr[:, out : out + latent] = even[:, :latent].astype(BF16)
        dq_scr[:, out + latent : out + 2 * latent] = odd[:, :latent].astype(BF16)
        turned = jnp.where(lane < rope, even[:, latent:], odd[:, latent:])
        dr_scr[:, 2 * p * rope : 2 * (p + 1) * rope] = turned.astype(BF16)
        cols = slice(out, out + 2 * latent)
        copies.append(pltpu.make_async_copy(dq_scr.at[:, cols], dq_ref.at[:, cols], sems.at[p]))
        copies[-1].start()
    copies.append(pltpu.make_async_copy(dr_scr, dr_ref, sems.at[pairs]))
    copies[-1].start()
    rows = slice(own * tokens, (own + 1) * tokens)
    main, turned = key_gradient(
        ds_ref[rows, :], w_ref[rows, :], q2_ref[...], u2_ref[...], latent
    )
    start = jnp.zeros(grad_ref.shape, F32)
    for ref in met_refs:
        is_odd = lax.rem(lax.axis_index("blk"), 2) == 1
        start = jnp.where(is_odd, start, ref[:tokens, :].astype(F32))
    grad_ref[:, :latent] = start[:, :latent] + main
    grad_ref[:, latent:] = start[:, latent:] + turned
    for copy in copies:
        copy.wait()


def per_device(query_latent, query_rotary, upstream, latent, key_rotary, pattern):
    blocks = lax.axis_size("blk")
    spacing = spacing_list(blocks)
    nd = len(spacing)
    inner = lax.axis_size("inner")
    tokens = query_latent.shape[0]
    shard, width = latent.shape
    rope = key_rotary.shape[1]
    heads = query_latent.shape[1] // width
    pairs = heads // 2
    wide = width + 2 * rope
    depth = nd * tokens
    rows = heads * tokens
    scale = (NOPE + rope) ** (-0.5)
    paired = spacing == [0, 1, 2, 3, 4] and blocks % 2 == 0

    hbm = pl.BlockSpec(memory_space=pltpu.HBM)
    vmem = pl.BlockSpec(memory_space=pltpu.VMEM)
    smem = pl.BlockSpec(memory_space=pltpu.SMEM)
    params = pltpu.CompilerParams(vmem_limit_bytes=VMEM)

    def staged(lanes, array, *ropes):
        return pl.pallas_call(
            functools.partial(stage_kernel, (heads, tokens, width, rope)),
            in_specs=[hbm] + [vmem] * len(ropes),
            out_specs=vmem,
            out_shape=jax.ShapeDtypeStruct((rows, lanes), BF16),
            scratch_shapes=[pltpu.SemaphoreType.DMA((heads,))],
            cost_estimate=pl.CostEstimate(
                flops=rows * lanes * width, bytes_accessed=4 * rows * lanes, transcendentals=0
            ),
            compiler_params=params,
        )(array, *ropes)

    q2 = staged(wide, query_latent, query_rotary)
    own = jnp.concatenate([latent, key_rotary, key_rotary], axis=1)
    gathered = [own] + [rotated(own, "inner", k) for k in range(1, inner)]
    gathered, q2 = lax.optimization_barrier((gathered, q2))
    near = jnp.concatenate(gathered, axis=0)
    u2 = staged(width, upstream)
    if paired:
        order = [4, 2, 0, 1, 3]
        kept = 3
        groups = [[1, 2], [0, 3]]
        two = rotated(near, "blk", 2)
        four = rotated(near, "blk", 4)
        near_met = swapped(near)
        two, u2 = lax.optimization_barrier((two, u2))
        two_met = swapped(two)
        sources = [(2,), (1,), (0,), (4, 3), (5, 4)]
    else:
        order = spacing
        kept = 1
        groups = [[0]]
        sources = [(d,) for d in range(nd)]
    sent = nd - kept
    entries = [spacing.index(d) for d in order]
    behind = depth - sum(len(group) for group in groups) * tokens

    def early_scores(group, key_arrays, sources):
        ahead = len(group) * tokens
        return pl.pallas_call(
            functools.partial(
                early_kernel,
                (pairs, tokens, shard, width, scale),
                sources,
                [entries[d] for d in group],
            ),
            in_specs=[smem] + [vmem] * (2 + len(key_arrays)),
            out_specs=[vmem] * 3,
            out_shape=[
                jax.ShapeDtypeStruct((ahead, rows), F32),
                jax.ShapeDtypeStruct((ahead, rows), F32),
                jax.ShapeDtypeStruct((8, rows), F32),
            ],
            scratch_shapes=[pltpu.VMEM((ahead, wide), BF16)],
            cost_estimate=pl.CostEstimate(
                flops=2 * rows * ahead * (wide + width),
                bytes_accessed=8 * rows * ahead,
                transcendentals=rows * ahead,
            ),
            compiler_params=params,
        )(pattern, q2, u2, *key_arrays)

    if paired:
        first = early_scores(groups[0], [two, near], [(0,), (1,)])
        four, first = lax.optimization_barrier((four, first))
        four_met = swapped(four)
        second = early_scores(groups[1], [four, near_met, two_met], [(0,), (2, 1)])
        early = [*first, *second]
        key_arrays = [near, two, four, near_met, two_met, four_met]
    else:
        early = early_scores(groups[0], [near], [(0,)])
        key_arrays = [near] + [rotated(near, "blk", d) for d in spacing[1:]]
    queries = (q2, u2)

    ds, weights, keys, grads = pl.pallas_call(
        functools.partial(
            scores_kernel, (nd, kept, pairs, tokens, width, scale), groups, sources, entries
        ),
        in_specs=[smem] + [vmem] * (2 + len(early) + len(key_arrays)),
        out_specs=[vmem] * 4,
        out_shape=[
            jax.ShapeDtypeStruct((depth, rows), BF16),
            jax.ShapeDtypeStruct((kept * tokens, rows), BF16),
            jax.ShapeDtypeStruct((depth, wide), BF16),
            jax.ShapeDtypeStruct((sent * tokens, wide), BF16),
        ],
        scratch_shapes=[
            pltpu.VMEM((behind, wide), BF16),
            pltpu.VMEM((2, behind, 2 * tokens), F32),
            pltpu.VMEM((2, behind, 2 * tokens), F32),
            pltpu.VMEM((sent * tokens, rows), BF16),
        ],
        cost_estimate=pl.CostEstimate(
            flops=2 * rows * (behind + sent * tokens) * (wide + width),
            bytes_accessed=8 * rows * depth,
            transcendentals=rows * behind,
        ),
        compiler_params=params,
        name="scores",
    )(pattern, *queries, *early, *key_arrays)

    if paired:
        met = swapped(grads)
        late = pl.pallas_call(
            functools.partial(gradient_kernel, ((kept - 1) * tokens, width)),
            out_shape=jax.ShapeDtypeStruct(((kept - 1) * tokens, wide), F32),
            cost_estimate=pl.CostEstimate(
                flops=2 * rows * (kept - 1) * tokens * (wide + width),
                bytes_accessed=4 * rows * wide,
                transcendentals=0,
            ),
            compiler_params=params,
            name="late_gradients",
        )(ds, weights, *queries)
        to_four, to_two = pl.pallas_call(
            merge_kernel,
            out_shape=[jax.ShapeDtypeStruct((tokens, wide), BF16)] * 2,
            compiler_params=params,
            name="merge",
        )(late, met)
        back = [rotated(to_two, "blk", -2), rotated(to_four, "blk", -4)]
        handed = [met]
    else:
        back = [
            rotated(grads[k * tokens : (k + 1) * tokens], "blk", -d)
            for k, d in enumerate(spacing[1:])
        ]
        handed = []

    own_grad, query_cotangent, rotary_cotangent = pl.pallas_call(
        functools.partial(own_kernel, (kept - 1, pairs, tokens, width, rope)),
        in_specs=[vmem] * (5 + len(handed)),
        out_specs=[vmem, hbm, hbm],
        out_shape=[
            jax.ShapeDtypeStruct((tokens, wide), F32),
            jax.ShapeDtypeStruct(query_latent.shape, BF16),
            jax.ShapeDtypeStruct(query_rotary.shape, BF16),
        ],
        scratch_shapes=[
            pltpu.VMEM(query_latent.shape, BF16),
            pltpu.VMEM(query_rotary.shape, BF16),
            pltpu.SemaphoreType.DMA((pairs + 1,)),
        ],
        cost_estimate=pl.CostEstimate(
            flops=2 * rows * (tokens * (wide + width) + depth * wide),
            bytes_accessed=2 * rows * (wide + depth),
            transcendentals=0,
        ),
        compiler_params=params,
        name="own_gradients",
    )(ds, weights, *queries, keys, *handed)

    parts = pl.pallas_call(
        functools.partial(total_kernel, len(back)),
        out_shape=[
            jax.ShapeDtypeStruct((shard, wide), F32 if k == 0 else BF16) for k in range(inner)
        ],
        compiler_params=params,
        name="total",
    )(own_grad, *back)
    moved = [rotated(parts[k], "inner", -k) for k in range(1, inner)]

    latent_cotangent, positional_cotangent = pl.pallas_call(
        functools.partial(finish_kernel, (width, rope)),
        out_shape=[
            jax.ShapeDtypeStruct((shard, width), F32),
            jax.ShapeDtypeStruct((shard, rope), F32),
        ],
        compiler_params=params,
        name="finish",
    )(parts[0], *moved)
    return (query_cotangent, rotary_cotangent, latent_cotangent, positional_cotangent)


def solution(mesh):
    in_specs = (
        P("blk", "inner"),
        P("blk", "inner"),
        P("blk", "inner"),
        P(("blk", "inner"), None),
        P(("blk", "inner"), None),
        P("blk", None),
    )
    out_specs = (
        P("blk", "inner"),
        P("blk", "inner"),
        P(("blk", "inner"), None),
        P(("blk", "inner"), None),
    )

    return jax.shard_map(per_device, mesh=mesh, in_specs=in_specs, out_specs=out_specs, check_vma=False)
```

profile of v0, /device:TPU:2, one launch (start us, length us, event | category | flops | bytes accessed | tf_op | source)
XLA Modules:
  0.0 44.7 jit_solution(7664607519453381358)
XLA Ops:
  0.6 0.9 %pad_maximum_fusion = bf16[32,640]{1,0:T(8,128)(2,1)S(1)} fusion(bf16[32,64]{1,0:T(8,128)(2,1)} %param.10, bf16[32,512]{1,0:T(8,128)(2,1)} %param.9), kind=kLoop, calls=%fused_computation | loop fusion | flops 122880 | bytes 77824 | tf_op jit(solution)/shard_map/concatenate | solution.py:298
  1.5 3.6 %collective-permute-start.2 = (bf16[32,640]{1,0:T(8,128)(2,1)S(1)}, bf16[32,640]{1,0:T(8,128)(2,1)S(1)}, u32[]{:S(2)}, u32[]{:S(2)}) collective-permute-start(bf16[32,640]{1,0:T(8,128)(2,1)S(1)} %pad_maximum_fusion), channel_id=1, source_target_pairs={{0,3},{1,0},{2,1},{3,2},{4,7},{5,4},{6,5},{7,6},{8,11},{9,8},{10,9... | collective-permute-start | bytes 122888 | tf_op jit(solution)/shard_map/ppermute | solution.py:31
  5.1 1.0 %collective-permute-start = (bf16[32,640]{1,0:T(8,128)(2,1)S(1)}, bf16[32,640]{1,0:T(8,128)(2,1)S(1)}, u32[]{:S(2)}, u32[]{:S(2)}) collective-permute-start(bf16[32,640]{1,0:T(8,128)(2,1)S(1)} %pad_maximum_fusion), channel_id=1, source_target_pairs={{0,1},{1,2},{2,3},{3,0},{4,5},{5,6},{6,7},{7,4},{8,9},{9,10},{10,1... | collective-permute-start | bytes 122888 | tf_op jit(solution)/shard_map/ppermute | solution.py:31
  6.1 1.2 %copy-done = bf16[128,4096]{1,0:T(8,128)(2,1)S(1)} copy-done((bf16[128,4096]{1,0:T(8,128)(2,1)S(1)}, bf16[128,4096]{1,0:T(8,128)(2,1)}, u32[]{:S(2)}) %copy-start) | copy-done | bytes 1048600
  7.3 0.9 %copy-done.2 = bf16[128,512]{1,0:T(8,128)(2,1)S(1)} copy-done((bf16[128,512]{1,0:T(8,128)(2,1)S(1)}, bf16[128,512]{1,0:T(8,128)(2,1)}, u32[]{:S(2)}) %copy-start.2) | copy-done | bytes 131096
  8.6 1.4 %collective-permute-done.1 = bf16[32,640]{1,0:T(8,128)(2,1)S(1)} collective-permute-done((bf16[32,640]{1,0:T(8,128)(2,1)S(1)}, bf16[32,640]{1,0:T(8,128)(2,1)S(1)}, u32[]{:S(2)}, u32[]{:S(2)}) %collective-permute-start.1) | collective-permute-done | bytes 40992 | tf_op jit(solution)/shard_map/ppermute | solution.py:31
  10.0 0.9 %collective-permute-done = bf16[32,640]{1,0:T(8,128)(2,1)S(1)} collective-permute-done((bf16[32,640]{1,0:T(8,128)(2,1)S(1)}, bf16[32,640]{1,0:T(8,128)(2,1)S(1)}, u32[]{:S(2)}, u32[]{:S(2)}) %collective-permute-start) | collective-permute-done | bytes 40992 | tf_op jit(solution)/shard_map/ppermute | solution.py:31
  11.0 1.5 %collective-permute-start.3 = (bf16[128,640]{1,0:T(8,128)(2,1)S(1)}, bf16[128,640]{1,0:T(8,128)(2,1)S(1)}, u32[]{:S(2)}, u32[]{:S(2)}) collective-permute-start(bf16[128,640]{1,0:T(8,128)(2,1)S(1)} %constant_dynamic-update-slice_fusion.refs_1_.refs_6_), channel_id=1, source_target_pairs={{0,8},{4,12},{8,16},{12,20},{16,24},{20,28},{24,0},{28,4},{1,9},{5... | collective-permute-start | bytes 491528 | tf_op jit(solution)/shard_map/ppermute | solution.py:31
  13.3 3.0 %collective-permute-done.3.refs_0_.refs_7_ = bf16[128,640]{1,0:T(8,128)(2,1)S(1)} collective-permute-done((bf16[128,640]{1,0:T(8,128)(2,1)S(1)}, bf16[128,640]{1,0:T(8,128)(2,1)S(1)}, u32[]{:S(2)}, u32[]{:S(2)}) %collective-permute-start.3) | collective-permute-done | bytes 163872 | tf_op jit(solution)/shard_map/ppermute | solution.py:31
  16.3 1.6 %shard_map.95 = (f32[256,1024]{1,0:T(8,128)S(1)}, f32[256,1024]{1,0:T(8,128)S(1)}, f32[8,1024]{1,0:T(8,128)S(1)}) custom-call(s32[1,5]{1,0:T(1,128)S(1)} %copy-done.3, bf16[1024,640]{1,0:T(8,128)(2,1)S(1)} %shard_map.93.q2_ref, bf16[1024,512]{1,0:T(8,128)(2,1)S(1)} %shard_map.94.u2_ref, bf16[128,640]{1,0:T(8,128)(2,1)S(1)} %collective-permute-done.3.refs_0_.refs_7_, ...), custom_call_target="tpu_custom_call" | custom-call | flops 603979776 | bytes 2097152 | tf_op jit(solution)/shard_map/pallas_call | solution.py:324
  18.5 1.6 %shard_map.96 = (f32[256,1024]{1,0:T(8,128)S(1)}, f32[256,1024]{1,0:T(8,128)S(1)}, f32[8,1024]{1,0:T(8,128)S(1)}) custom-call(s32[1,5]{1,0:T(1,128)S(1)} %copy-done.3, bf16[1024,640]{1,0:T(8,128)(2,1)S(1)} %shard_map.93.q2_ref, bf16[1024,512]{1,0:T(8,128)(2,1)S(1)} %shard_map.94.u2_ref, bf16[128,640]{1,0:T(8,128)(2,1)S(1)} %collective-permute-done.4.refs_0_.refs_8_, ...), custom_call_target="tpu_custom_call" | custom-call | flops 603979776 | bytes 2097152 | tf_op jit(solution)/shard_map/pallas_call | solution.py:324
  20.2 2.6 %scores.1 = (bf16[640,1024]{1,0:T(8,128)(2,1)S(1)}, bf16[384,1024]{1,0:T(8,128)(2,1)S(1)}, bf16[640,640]{1,0:T(8,128)(2,1)S(1)}, bf16[256,640]{1,0:T(8,128)(2,1)S(1)}) custom-call(s32[1,5]{1,0:T(1,128)S(1)} %copy-done.3, bf16[1024,640]{1,0:T(8,128)(2,1)S(1)} %shard_map.93.q2_ref, bf16[1024,512]{1,0:T(8,128)(2,1)S(1)} %shard_map.94.u2_ref, ...), custom_call_target="tpu_custom_call" | custom-call | flops 905969664 | bytes 5242880 | tf_op jit(solution)/shard_map/scores/pallas_call | solution.py:359
  22.9 0.8 %late_gradients.1.late_ref = f32[256,640]{1,0:T(8,128)S(1)} custom-call(bf16[640,1024]{1,0:T(8,128)(2,1)S(1)} %get-tuple-element.53.ds_ref, bf16[384,1024]{1,0:T(8,128)(2,1)S(1)} %get-tuple-element.54.w_ref, bf16[1024,640]{1,0:T(8,128)(2,1)S(1)} %shard_map.93.q2_ref, bf16[1024,512]{1,0:T(8,128)(2,1)S(1)} %shard_map.94.u2_ref), custom_call_target="tpu_custom_call" | custom-call | flops 603979776 | bytes 2621440 | tf_op jit(solution)/shard_map/late_gradients/pallas_call | solution.py:388
  23.7 0.8 %collective-permute-done.8.refs_0_.met_ref = bf16[256,640]{1,0:T(8,128)(2,1)S(1)} collective-permute-done((bf16[256,640]{1,0:T(8,128)(2,1)S(1)}, bf16[256,640]{1,0:T(8,128)(2,1)S(1)}, u32[]{:S(2)}, u32[]{:S(2)}) %collective-permute-start.8) | collective-permute-done | bytes 327712 | tf_op jit(solution)/shard_map/ppermute | solution.py:36
  24.6 2.1 %collective-permute-start.9 = (bf16[128,640]{1,0:T(8,128)(2,1)S(1)}, bf16[128,640]{1,0:T(8,128)(2,1)S(1)}, u32[]{:S(2)}, u32[]{:S(2)}) collective-permute-start(bf16[128,640]{1,0:T(8,128)(2,1)S(1)} %get-tuple-element.60), channel_id=1, source_target_pairs={{0,24},{4,28},{8,0},{12,4},{16,8},{20,12},{24,16},{28,20},{1,25},{... | collective-permute-start | bytes 491528 | tf_op jit(solution)/shard_map/ppermute | solution.py:31
  26.7 1.5 %collective-permute-start.10 = (bf16[128,640]{1,0:T(8,128)(2,1)S(1)}, bf16[128,640]{1,0:T(8,128)(2,1)S(1)}, u32[]{:S(2)}, u32[]{:S(2)}) collective-permute-start(bf16[128,640]{1,0:T(8,128)(2,1)S(1)} %get-tuple-element.61), channel_id=1, source_target_pairs={{0,16},{4,20},{8,24},{12,28},{16,0},{20,4},{24,8},{28,12},{1,17},{... | collective-permute-start | bytes 491528 | tf_op jit(solution)/shard_map/ppermute | solution.py:31
  28.2 2.3 %own_gradients.1 = (f32[128,640]{1,0:T(8,128)S(1)}, bf16[128,4096]{1,0:T(8,128)(2,1)}, bf16[128,512]{1,0:T(8,128)(2,1)}) custom-call(bf16[640,1024]{1,0:T(8,128)(2,1)S(1)} %get-tuple-element.53.ds_ref, bf16[384,1024]{1,0:T(8,128)(2,1)S(1)} %get-tuple-element.54.w_ref, bf16[1024,640]{1,0:T(8,128)(2,1)S(1)} %shard_map.93.q2_ref, ...), custom_call_target="tpu_custom_call" | custom-call | flops 1140850688 | bytes 2621440 | tf_op jit(solution)/shard_map/own_gradients/pallas_call | solution.py:414
  30.5 2.0 %collective-permute-done.9.refs_0_ = bf16[128,640]{1,0:T(8,128)(2,1)S(1)} collective-permute-done((bf16[128,640]{1,0:T(8,128)(2,1)S(1)}, bf16[128,640]{1,0:T(8,128)(2,1)S(1)}, u32[]{:S(2)}, u32[]{:S(2)}) %collective-permute-start.9) | collective-permute-done | bytes 163872 | tf_op jit(solution)/shard_map/ppermute | solution.py:31
  32.5 3.4 %collective-permute-done.10.refs_1_ = bf16[128,640]{1,0:T(8,128)(2,1)S(1)} collective-permute-done((bf16[128,640]{1,0:T(8,128)(2,1)S(1)}, bf16[128,640]{1,0:T(8,128)(2,1)S(1)}, u32[]{:S(2)}, u32[]{:S(2)}) %collective-permute-start.10) | collective-permute-done | bytes 163872 | tf_op jit(solution)/shard_map/ppermute | solution.py:31
  36.0 1.4 %collective-permute-start.11 = (bf16[32,640]{1,0:T(8,128)(2,1)S(1)}, bf16[32,640]{1,0:T(8,128)(2,1)S(1)}, u32[]{:S(2)}, u32[]{:S(2)}) collective-permute-start(bf16[32,640]{1,0:T(8,128)(2,1)S(1)} %get-tuple-element.63), channel_id=1, source_target_pairs={{0,3},{1,0},{2,1},{3,2},{4,7},{5,4},{6,5},{7,6},{8,11},{9,8},{10,9... | collective-permute-start | bytes 122888 | tf_op jit(solution)/shard_map/ppermute | solution.py:31
  37.4 0.8 %collective-permute-start.12 = (bf16[32,640]{1,0:T(8,128)(2,1)S(1)}, bf16[32,640]{1,0:T(8,128)(2,1)S(1)}, u32[]{:S(2)}, u32[]{:S(2)}) collective-permute-start(bf16[32,640]{1,0:T(8,128)(2,1)S(1)} %get-tuple-element.64), channel_id=1, source_target_pairs={{0,2},{1,3},{2,0},{3,1},{4,6},{5,7},{6,4},{7,5},{8,10},{9,11},{10,... | collective-permute-start | bytes 122888 | tf_op jit(solution)/shard_map/ppermute | solution.py:31
  38.2 1.4 %collective-permute-start.13 = (bf16[32,640]{1,0:T(8,128)(2,1)S(1)}, bf16[32,640]{1,0:T(8,128)(2,1)S(1)}, u32[]{:S(2)}, u32[]{:S(2)}) collective-permute-start(bf16[32,640]{1,0:T(8,128)(2,1)S(1)} %get-tuple-element.65), channel_id=1, source_target_pairs={{0,1},{1,2},{2,3},{3,0},{4,5},{5,6},{6,7},{7,4},{8,9},{9,10},{10,1... | collective-permute-start | bytes 122888 | tf_op jit(solution)/shard_map/ppermute | solution.py:31
  40.0 3.1 %collective-permute-done.12.refs_1_ = bf16[32,640]{1,0:T(8,128)(2,1)S(1)} collective-permute-done((bf16[32,640]{1,0:T(8,128)(2,1)S(1)}, bf16[32,640]{1,0:T(8,128)(2,1)S(1)}, u32[]{:S(2)}, u32[]{:S(2)}) %collective-permute-start.12) | collective-permute-done | bytes 40992 | tf_op jit(solution)/shard_map/ppermute | solution.py:31
  43.2 0.9 %collective-permute-done.13.refs_2_ = bf16[32,640]{1,0:T(8,128)(2,1)S(1)} collective-permute-done((bf16[32,640]{1,0:T(8,128)(2,1)S(1)}, bf16[32,640]{1,0:T(8,128)(2,1)S(1)}, u32[]{:S(2)}, u32[]{:S(2)}) %collective-permute-start.13) | collective-permute-done | bytes 40992 | tf_op jit(solution)/shard_map/ppermute | solution.py:31
  (27 shorter events, 3.1 us)
Async XLA Ops:
  1.5 7.0 %collective-permute-start.2 = (bf16[32,640]{1,0:T(8,128)(2,1)S(1)}, bf16[32,640]{1,0:T(8,128)(2,1)S(1)}, u32[]{:S(2)}, u32[]{:S(2)}) collective-permute-start(bf16[32,640]{1,0:T(8,128)(2,1)S(1)} %pad_maximum_fusion), channel_id=1, source_target_pairs={{0,3},{1,0},{2,1},{3,2},{4,7},{5,4},{6,5},{7,6},{8,11},{9,8},{10,9... | collective-permute-start | bytes 122888 | tf_op jit(solution)/shard_map/ppermute | solution.py:31
  5.1 4.9 %collective-permute-start.1 = (bf16[32,640]{1,0:T(8,128)(2,1)S(1)}, bf16[32,640]{1,0:T(8,128)(2,1)S(1)}, u32[]{:S(2)}, u32[]{:S(2)}) collective-permute-start(bf16[32,640]{1,0:T(8,128)(2,1)S(1)} %pad_maximum_fusion), channel_id=1, source_target_pairs={{0,2},{1,3},{2,0},{3,1},{4,6},{5,7},{6,4},{7,5},{8,10},{9,11},{10,... | collective-permute-start | bytes 122888 | tf_op jit(solution)/shard_map/ppermute | solution.py:31
  5.1 5.8 %collective-permute-start = (bf16[32,640]{1,0:T(8,128)(2,1)S(1)}, bf16[32,640]{1,0:T(8,128)(2,1)S(1)}, u32[]{:S(2)}, u32[]{:S(2)}) collective-permute-start(bf16[32,640]{1,0:T(8,128)(2,1)S(1)} %pad_maximum_fusion), channel_id=1, source_target_pairs={{0,1},{1,2},{2,3},{3,0},{4,5},{5,6},{6,7},{7,4},{8,9},{9,10},{10,1... | collective-permute-start | bytes 122888 | tf_op jit(solution)/shard_map/ppermute | solution.py:31
  6.1 1.2 %copy-start = (bf16[128,4096]{1,0:T(8,128)(2,1)S(1)}, bf16[128,4096]{1,0:T(8,128)(2,1)}, u32[]{:S(2)}) copy-start(bf16[128,4096]{1,0:T(8,128)(2,1)} %x_ref.2) | copy-start | bytes 3145732
  7.3 0.9 %copy-start.2 = (bf16[128,512]{1,0:T(8,128)(2,1)S(1)}, bf16[128,512]{1,0:T(8,128)(2,1)}, u32[]{:S(2)}) copy-start(bf16[128,512]{1,0:T(8,128)(2,1)} %refs_0_.1) | copy-start | bytes 393220
  8.2 4.8 %copy-start.1 = (bf16[128,4096]{1,0:T(8,128)(2,1)S(1)}, bf16[128,4096]{1,0:T(8,128)(2,1)}, u32[]{:S(2)}) copy-start(bf16[128,4096]{1,0:T(8,128)(2,1)} %x_ref.3) | copy-start | bytes 3145732
  8.5 7.8 %copy-start.3 = (s32[1,5]{1,0:T(1,128)S(1)}, s32[1,5]{1,0:T(1,128)}, u32[]{:S(2)}) copy-start(s32[1,5]{1,0:T(1,128)} %pattern_ref.5) | copy-start | bytes 64
  11.0 5.4 %collective-permute-start.3 = (bf16[128,640]{1,0:T(8,128)(2,1)S(1)}, bf16[128,640]{1,0:T(8,128)(2,1)S(1)}, u32[]{:S(2)}, u32[]{:S(2)}) collective-permute-start(bf16[128,640]{1,0:T(8,128)(2,1)S(1)} %constant_dynamic-update-slice_fusion.refs_1_.refs_6_), channel_id=1, source_target_pairs={{0,8},{4,12},{8,16},{12,20},{16,24},{20,28},{24,0},{28,4},{1,9},{5... | collective-permute-start | bytes 491528 | tf_op jit(solution)/shard_map/ppermute | solution.py:31
  12.5 5.5 %collective-permute-start.4 = (bf16[128,640]{1,0:T(8,128)(2,1)S(1)}, bf16[128,640]{1,0:T(8,128)(2,1)S(1)}, u32[]{:S(2)}, u32[]{:S(2)}) collective-permute-start(bf16[128,640]{1,0:T(8,128)(2,1)S(1)} %constant_dynamic-update-slice_fusion.refs_1_.refs_6_), channel_id=1, source_target_pairs={{0,16},{4,20},{8,24},{12,28},{16,0},{20,4},{24,8},{28,12},{1,17},{... | collective-permute-start | bytes 491528 | tf_op jit(solution)/shard_map/ppermute | solution.py:31
  13.2 5.3 %collective-permute-start.5 = (bf16[128,640]{1,0:T(8,128)(2,1)S(1)}, bf16[128,640]{1,0:T(8,128)(2,1)S(1)}, u32[]{:S(2)}, u32[]{:S(2)}) collective-permute-start(bf16[128,640]{1,0:T(8,128)(2,1)S(1)} %constant_dynamic-update-slice_fusion.refs_1_.refs_6_), channel_id=1, source_target_pairs={{0,4},{4,0},{8,12},{12,8},{16,20},{20,16},{24,28},{28,24},{1,5},{5... | collective-permute-start | bytes 491528 | tf_op jit(solution)/shard_map/ppermute | solution.py:36
  16.3 2.2 %collective-permute-start.6 = (bf16[128,640]{1,0:T(8,128)(2,1)S(1)}, bf16[128,640]{1,0:T(8,128)(2,1)S(1)}, u32[]{:S(2)}, u32[]{:S(2)}) collective-permute-start(bf16[128,640]{1,0:T(8,128)(2,1)S(1)} %collective-permute-done.3.refs_0_.refs_7_), channel_id=1, source_target_pairs={{0,4},{4,0},{8,12},{12,8},{16,20},{20,16},{24,28},{28,24},{1,5},{5... | collective-permute-start | bytes 491528 | tf_op jit(solution)/shard_map/ppermute | solution.py:36
  18.0 2.2 %collective-permute-start.7 = (bf16[128,640]{1,0:T(8,128)(2,1)S(1)}, bf16[128,640]{1,0:T(8,128)(2,1)S(1)}, u32[]{:S(2)}, u32[]{:S(2)}) collective-permute-start(bf16[128,640]{1,0:T(8,128)(2,1)S(1)} %collective-permute-done.4.refs_0_.refs_8_), channel_id=1, source_target_pairs={{0,4},{4,0},{8,12},{12,8},{16,20},{20,16},{24,28},{28,24},{1,5},{5... | collective-permute-start | bytes 491528 | tf_op jit(solution)/shard_map/ppermute | solution.py:36
  22.8 1.7 %collective-permute-start.8 = (bf16[256,640]{1,0:T(8,128)(2,1)S(1)}, bf16[256,640]{1,0:T(8,128)(2,1)S(1)}, u32[]{:S(2)}, u32[]{:S(2)}) collective-permute-start(bf16[256,640]{1,0:T(8,128)(2,1)S(1)} %get-tuple-element.56), channel_id=1, source_target_pairs={{0,4},{4,0},{8,12},{12,8},{16,20},{20,16},{24,28},{28,24},{1,5},{5... | collective-permute-start | bytes 983048 | tf_op jit(solution)/shard_map/ppermute | solution.py:36
  24.6 7.9 %collective-permute-start.9 = (bf16[128,640]{1,0:T(8,128)(2,1)S(1)}, bf16[128,640]{1,0:T(8,128)(2,1)S(1)}, u32[]{:S(2)}, u32[]{:S(2)}) collective-permute-start(bf16[128,640]{1,0:T(8,128)(2,1)S(1)} %get-tuple-element.60), channel_id=1, source_target_pairs={{0,24},{4,28},{8,0},{12,4},{16,8},{20,12},{24,16},{28,20},{1,25},{... | collective-permute-start | bytes 491528 | tf_op jit(solution)/shard_map/ppermute | solution.py:31
  26.7 9.2 %collective-permute-start.10 = (bf16[128,640]{1,0:T(8,128)(2,1)S(1)}, bf16[128,640]{1,0:T(8,128)(2,1)S(1)}, u32[]{:S(2)}, u32[]{:S(2)}) collective-permute-start(bf16[128,640]{1,0:T(8,128)(2,1)S(1)} %get-tuple-element.61), channel_id=1, source_target_pairs={{0,16},{4,20},{8,24},{12,28},{16,0},{20,4},{24,8},{28,12},{1,17},{... | collective-permute-start | bytes 491528 | tf_op jit(solution)/shard_map/ppermute | solution.py:31
  36.0 4.1 %collective-permute-start.11 = (bf16[32,640]{1,0:T(8,128)(2,1)S(1)}, bf16[32,640]{1,0:T(8,128)(2,1)S(1)}, u32[]{:S(2)}, u32[]{:S(2)}) collective-permute-start(bf16[32,640]{1,0:T(8,128)(2,1)S(1)} %get-tuple-element.63), channel_id=1, source_target_pairs={{0,3},{1,0},{2,1},{3,2},{4,7},{5,4},{6,5},{7,6},{8,11},{9,8},{10,9... | collective-permute-start | bytes 122888 | tf_op jit(solution)/shard_map/ppermute | solution.py:31
  37.4 5.8 %collective-permute-start.12 = (bf16[32,640]{1,0:T(8,128)(2,1)S(1)}, bf16[32,640]{1,0:T(8,128)(2,1)S(1)}, u32[]{:S(2)}, u32[]{:S(2)}) collective-permute-start(bf16[32,640]{1,0:T(8,128)(2,1)S(1)} %get-tuple-element.64), channel_id=1, source_target_pairs={{0,2},{1,3},{2,0},{3,1},{4,6},{5,7},{6,4},{7,5},{8,10},{9,11},{10,... | collective-permute-start | bytes 122888 | tf_op jit(solution)/shard_map/ppermute | solution.py:31
  38.2 5.8 %collective-permute-start.13 = (bf16[32,640]{1,0:T(8,128)(2,1)S(1)}, bf16[32,640]{1,0:T(8,128)(2,1)S(1)}, u32[]{:S(2)}, u32[]{:S(2)}) collective-permute-start(bf16[32,640]{1,0:T(8,128)(2,1)S(1)} %get-tuple-element.65), channel_id=1, source_target_pairs={{0,1},{1,2},{2,3},{3,0},{4,5},{5,6},{6,7},{7,4},{8,9},{9,10},{10,1... | collective-permute-start | bytes 122888 | tf_op jit(solution)/shard_map/ppermute | solution.py:31
where the time goes:
time: 45 us; the launch traced here: 44.7 us
  waiting for transfers between devices  16 us (36%)
  starting transfers between devices  14.7 us (33%)
  Pallas kernels  10.3 us (23%)
  local copies, waits for them, and re-layouts  2.18 us (5%)
  other arithmetic  0.87 us (2%)
  between operations  0.75 us (2%)
    ppermute x10, waiting for transfers between devices, rotated(): lax.ppermute(value, axis, [(s, (s + steps) % count) for s in range(count)])  15.2 us
    ppermute x10, starting transfers between devices, rotated(): lax.ppermute(value, axis, [(s, (s + steps) % count) for s in range(count)])  13.9 us
    pallas_call x2, Pallas kernels, early_scores(): pl.pallas_call(functools.partial(early_kernel, (pairs, tokens, shard, wid...  3.2 us
    pallas_call x1, Pallas kernels, per_device(): pl.pallas_call(functools.partial(scores_kernel, (nd, kept, pairs, tokens,...  2.63 us
    pallas_call x1, Pallas kernels, per_device(): pl.pallas_call(functools.partial(own_kernel, (kept - 1, pairs, tokens, wi...  2.26 us
    unnamed x11, local copies, waits for them, and re-layouts  2.16 us
  transfers between devices with their start and end apart: 14, of which 9 were waited for; matrix products, arithmetic and copies ran while one was open for 0% of the time, Pallas kernels for 15%

commit v1 on v0

--- a/solution.py
+++ b/solution.py
@@ -64,12 +64,23 @@
         copy.wait()
 
 
-def merge_kernel(late_ref, met_ref, four_ref, two_ref):
+def merge_kernel(late_ref, met_ref, two_ref, *four_refs):
     tokens = two_ref.shape[0]
     odd = lax.rem(lax.axis_index("blk"), 2) == 1
     one, three = met_ref[:tokens].astype(F32), met_ref[tokens:].astype(F32)
-    four_ref[...] = (late_ref[:tokens] + jnp.where(odd, three, 0.0)).astype(BF16)
     two_ref[...] = (late_ref[tokens:] + jnp.where(odd, one, three)).astype(BF16)
+    four = late_ref[:tokens] + jnp.where(odd, three, 0.0)
+    for k, ref in enumerate(four_refs):
+        shard = ref.shape[0]
+        ref[...] = four[k * shard : (k + 1) * shard].astype(ref.dtype)
+
+
+def sum_kernel(first_ref, *refs):
+    *part_refs, out_ref = refs
+    total = first_ref[...]
+    for ref in part_refs:
+        total += ref[...].astype(F32)
+    out_ref[...] = total.astype(out_ref.dtype)
 
 
 def total_kernel(returned, own_ref, *refs):
@@ -383,6 +394,9 @@
         name="scores",
     )(pattern, *queries, *early, *key_arrays)
 
+    part_shapes = [
+        jax.ShapeDtypeStruct((shard, wide), F32 if k == 0 else BF16) for k in range(inner)
+    ]
     if paired:
         met = swapped(grads)
         late = pl.pallas_call(
@@ -396,13 +410,21 @@
             compiler_params=params,
             name="late_gradients",
         )(ds, weights, *queries)
-        to_four, to_two = pl.pallas_call(
+        to_two, *four_parts = pl.pallas_call(
             merge_kernel,
-            out_shape=[jax.ShapeDtypeStruct((tokens, wide), BF16)] * 2,
+            out_shape=[jax.ShapeDtypeStruct((tokens, wide), BF16)] + part_shapes,
             compiler_params=params,
             name="merge",
         )(late, met)
-        back = [rotated(to_two, "blk", -2), rotated(to_four, "blk", -4)]
+        back = [rotated(to_two, "blk", -2)]
+        four_moved = [rotated(four_parts[k], "inner", -k) for k in range(1, inner)]
+        four_shard = pl.pallas_call(
+            sum_kernel,
+            out_shape=jax.ShapeDtypeStruct((shard, wide), BF16),
+            compiler_params=params,
+            name="sum_four",
+        )(four_parts[0], *four_moved)
+        shards_back = [rotated(four_shard, "blk", -4)]
         handed = [met]
     else:
         back = [
@@ -410,6 +432,7 @@
             for k, d in enumerate(spacing[1:])
         ]
         handed = []
+        shards_back = []
 
     own_grad, query_cotangent, rotary_cotangent = pl.pallas_call(
         functools.partial(own_kernel, (kept - 1, pairs, tokens, width, rope)),
@@ -436,9 +459,7 @@
 
     parts = pl.pallas_call(
         functools.partial(total_kernel, len(back)),
-        out_shape=[
-            jax.ShapeDtypeStruct((shard, wide), F32 if k == 0 else BF16) for k in range(inner)
-        ],
+        out_shape=part_shapes,
         compiler_params=params,
         name="total",
     )(own_grad, *back)
@@ -452,7 +473,7 @@
         ],
         compiler_params=params,
         name="finish",
-    )(parts[0], *moved)
+    )(parts[0], *moved, *shards_back)
     return (query_cotangent, rotary_cotangent, latent_cotangent, positional_cotangent)
 
 

time: 45 us -> 45.2 us (level)
  the two profiles are of different devices: /device:TPU:2 before, /device:TPU:0 now
where the time goes in v1:
time: 45.2 us; the launch traced here: 45 us
  starting transfers between devices  18.1 us (40%)
  waiting for transfers between devices  12.8 us (28%)
  Pallas kernels  10.3 us (23%)
  local copies, waits for them, and re-layouts  2.18 us (5%)
  other arithmetic  0.87 us (2%)
  between operations  0.76 us (2%)
    ppermute x13, starting transfers between devices, rotated(): lax.ppermute(value, axis, [(s, (s + steps) % count) for s in range(count)])  17.5 us
    ppermute x13, waiting for transfers between devices, rotated(): lax.ppermute(value, axis, [(s, (s + steps) % count) for s in range(count)])  12.4 us
    pallas_call x2, Pallas kernels, early_scores(): pl.pallas_call(functools.partial(early_kernel, (pairs, tokens, shard, wid...  3.21 us
    pallas_call x1, Pallas kernels, per_device(): pl.pallas_call(functools.partial(scores_kernel, (nd, kept, pairs, tokens,...  2.63 us
    pallas_call x1, Pallas kernels, per_device(): pl.pallas_call(functools.partial(own_kernel, (kept - 1, pairs, tokens, wi...  2.26 us
    unnamed x11, local copies, waits for them, and re-layouts  2.16 us
  transfers between devices with their start and end apart: 17, of which 10 were waited for; matrix products, arithmetic and copies ran while one was open for 0% of the time, Pallas kernels for 15%

profile of v1, /device:TPU:0, one launch (start us, length us, event | category | flops | bytes accessed | tf_op | source)
XLA Modules:
  0.0 45.0 jit_solution(5191327423024920791)
XLA Ops:
  1.5 5.1 %collective-permute-start.2 = (bf16[32,640]{1,0:T(8,128)(2,1)S(1)}, bf16[32,640]{1,0:T(8,128)(2,1)S(1)}, u32[]{:S(2)}, u32[]{:S(2)}) collective-permute-start(bf16[32,640]{1,0:T(8,128)(2,1)S(1)} %pad_maximum_fusion), channel_id=1, source_target_pairs={{0,3},{1,0},{2,1},{3,2},{4,7},{5,4},{6,5},{7,6},{8,11},{9,8},{10,9... | collective-permute-start | bytes 122888 | tf_op jit(solution)/shard_map/ppermute | solution.py:31
  6.6 1.0 %collective-permute-start = (bf16[32,640]{1,0:T(8,128)(2,1)S(1)}, bf16[32,640]{1,0:T(8,128)(2,1)S(1)}, u32[]{:S(2)}, u32[]{:S(2)}) collective-permute-start(bf16[32,640]{1,0:T(8,128)(2,1)S(1)} %pad_maximum_fusion), channel_id=1, source_target_pairs={{0,1},{1,2},{2,3},{3,0},{4,5},{5,6},{6,7},{7,4},{8,9},{9,10},{10,1... | collective-permute-start | bytes 122888 | tf_op jit(solution)/shard_map/ppermute | solution.py:31
  7.6 1.2 %copy-done = bf16[128,4096]{1,0:T(8,128)(2,1)S(1)} copy-done((bf16[128,4096]{1,0:T(8,128)(2,1)S(1)}, bf16[128,4096]{1,0:T(8,128)(2,1)}, u32[]{:S(2)}) %copy-start) | copy-done | bytes 1048600
  8.8 0.9 %copy-done.2 = bf16[128,512]{1,0:T(8,128)(2,1)S(1)} copy-done((bf16[128,512]{1,0:T(8,128)(2,1)S(1)}, bf16[128,512]{1,0:T(8,128)(2,1)}, u32[]{:S(2)}) %copy-start.2) | copy-done | bytes 131096
  10.0 1.4 %collective-permute-done.1 = bf16[32,640]{1,0:T(8,128)(2,1)S(1)} collective-permute-done((bf16[32,640]{1,0:T(8,128)(2,1)S(1)}, bf16[32,640]{1,0:T(8,128)(2,1)S(1)}, u32[]{:S(2)}, u32[]{:S(2)}) %collective-permute-start.1) | collective-permute-done | bytes 40992 | tf_op jit(solution)/shard_map/ppermute | solution.py:31
  11.5 0.9 %collective-permute-done = bf16[32,640]{1,0:T(8,128)(2,1)S(1)} collective-permute-done((bf16[32,640]{1,0:T(8,128)(2,1)S(1)}, bf16[32,640]{1,0:T(8,128)(2,1)S(1)}, u32[]{:S(2)}, u32[]{:S(2)}) %collective-permute-start) | collective-permute-done | bytes 40992 | tf_op jit(solution)/shard_map/ppermute | solution.py:31
  12.4 1.5 %collective-permute-start.3 = (bf16[128,640]{1,0:T(8,128)(2,1)S(1)}, bf16[128,640]{1,0:T(8,128)(2,1)S(1)}, u32[]{:S(2)}, u32[]{:S(2)}) collective-permute-start(bf16[128,640]{1,0:T(8,128)(2,1)S(1)} %constant_dynamic-update-slice_fusion.refs_1_.refs_6_), channel_id=1, source_target_pairs={{0,8},{4,12},{8,16},{12,20},{16,24},{20,28},{24,0},{28,4},{1,9},{5... | collective-permute-start | bytes 491528 | tf_op jit(solution)/shard_map/ppermute | solution.py:31
  14.0 1.5 %collective-permute-start.4 = (bf16[128,640]{1,0:T(8,128)(2,1)S(1)}, bf16[128,640]{1,0:T(8,128)(2,1)S(1)}, u32[]{:S(2)}, u32[]{:S(2)}) collective-permute-start(bf16[128,640]{1,0:T(8,128)(2,1)S(1)} %constant_dynamic-update-slice_fusion.refs_1_.refs_6_), channel_id=1, source_target_pairs={{0,16},{4,20},{8,24},{12,28},{16,0},{20,4},{24,8},{28,12},{1,17},{... | collective-permute-start | bytes 491528 | tf_op jit(solution)/shard_map/ppermute | solution.py:31
  15.8 3.0 %collective-permute-done.3.refs_0_.refs_7_ = bf16[128,640]{1,0:T(8,128)(2,1)S(1)} collective-permute-done((bf16[128,640]{1,0:T(8,128)(2,1)S(1)}, bf16[128,640]{1,0:T(8,128)(2,1)S(1)}, u32[]{:S(2)}, u32[]{:S(2)}) %collective-permute-start.3) | collective-permute-done | bytes 163872 | tf_op jit(solution)/shard_map/ppermute | solution.py:31
  18.8 1.6 %shard_map.95 = (f32[256,1024]{1,0:T(8,128)S(1)}, f32[256,1024]{1,0:T(8,128)S(1)}, f32[8,1024]{1,0:T(8,128)S(1)}) custom-call(s32[1,5]{1,0:T(1,128)S(1)} %copy-done.3, bf16[1024,640]{1,0:T(8,128)(2,1)S(1)} %shard_map.93.q2_ref, bf16[1024,512]{1,0:T(8,128)(2,1)S(1)} %shard_map.94.u2_ref, bf16[128,640]{1,0:T(8,128)(2,1)S(1)} %collective-permute-done.3.refs_0_.refs_7_, ...), custom_call_target="tpu_custom_call" | custom-call | flops 603979776 | bytes 2097152 | tf_op jit(solution)/shard_map/pallas_call | solution.py:335
  20.4 1.0 %collective-permute-done.4.refs_0_.refs_8_ = bf16[128,640]{1,0:T(8,128)(2,1)S(1)} collective-permute-done((bf16[128,640]{1,0:T(8,128)(2,1)S(1)}, bf16[128,640]{1,0:T(8,128)(2,1)S(1)}, u32[]{:S(2)}, u32[]{:S(2)}) %collective-permute-start.4) | collective-permute-done | bytes 163872 | tf_op jit(solution)/shard_map/ppermute | solution.py:31
  21.4 1.6 %shard_map.96 = (f32[256,1024]{1,0:T(8,128)S(1)}, f32[256,1024]{1,0:T(8,128)S(1)}, f32[8,1024]{1,0:T(8,128)S(1)}) custom-call(s32[1,5]{1,0:T(1,128)S(1)} %copy-done.3, bf16[1024,640]{1,0:T(8,128)(2,1)S(1)} %shard_map.93.q2_ref, bf16[1024,512]{1,0:T(8,128)(2,1)S(1)} %shard_map.94.u2_ref, bf16[128,640]{1,0:T(8,128)(2,1)S(1)} %collective-permute-done.4.refs_0_.refs_8_, ...), custom_call_target="tpu_custom_call" | custom-call | flops 603979776 | bytes 2097152 | tf_op jit(solution)/shard_map/pallas_call | solution.py:335
  23.0 2.6 %scores.1 = (bf16[640,1024]{1,0:T(8,128)(2,1)S(1)}, bf16[384,1024]{1,0:T(8,128)(2,1)S(1)}, bf16[640,640]{1,0:T(8,128)(2,1)S(1)}, bf16[256,640]{1,0:T(8,128)(2,1)S(1)}) custom-call(s32[1,5]{1,0:T(1,128)S(1)} %copy-done.3, bf16[1024,640]{1,0:T(8,128)(2,1)S(1)} %shard_map.93.q2_ref, bf16[1024,512]{1,0:T(8,128)(2,1)S(1)} %shard_map.94.u2_ref, ...), custom_call_target="tpu_custom_call" | custom-call | flops 905969664 | bytes 5242880 | tf_op jit(solution)/shard_map/scores/pallas_call | solution.py:370
  27.6 1.0 %collective-permute-start.9 = (bf16[128,640]{1,0:T(8,128)(2,1)S(1)}, bf16[128,640]{1,0:T(8,128)(2,1)S(1)}, u32[]{:S(2)}, u32[]{:S(2)}) collective-permute-start(bf16[128,640]{1,0:T(8,128)(2,1)S(1)} %get-tuple-element.63), channel_id=1, source_target_pairs={{0,24},{4,28},{8,0},{12,4},{16,8},{20,12},{24,16},{28,20},{1,25},{... | collective-permute-start | bytes 491528 | tf_op jit(solution)/shard_map/ppermute | solution.py:31
  29.2 1.0 %collective-permute-start.14 = (bf16[32,640]{1,0:T(8,128)(2,1)S(1)}, bf16[32,640]{1,0:T(8,128)(2,1)S(1)}, u32[]{:S(2)}, u32[]{:S(2)}) collective-permute-start(bf16[32,640]{1,0:T(8,128)(2,1)S(1)} %get-tuple-element.70), channel_id=1, source_target_pairs={{0,2},{1,3},{2,0},{3,1},{4,6},{5,7},{6,4},{7,5},{8,10},{9,11},{10,... | collective-permute-start | bytes 122888 | tf_op jit(solution)/shard_map/ppermute | solution.py:31
  30.2 1.5 %collective-permute-start.15 = (bf16[32,640]{1,0:T(8,128)(2,1)S(1)}, bf16[32,640]{1,0:T(8,128)(2,1)S(1)}, u32[]{:S(2)}, u32[]{:S(2)}) collective-permute-start(bf16[32,640]{1,0:T(8,128)(2,1)S(1)} %get-tuple-element.71), channel_id=1, source_target_pairs={{0,1},{1,2},{2,3},{3,0},{4,5},{5,6},{6,7},{7,4},{8,9},{9,10},{10,1... | collective-permute-start | bytes 122888 | tf_op jit(solution)/shard_map/ppermute | solution.py:31
  31.7 2.3 %own_gradients.1 = (f32[128,640]{1,0:T(8,128)S(1)}, bf16[128,4096]{1,0:T(8,128)(2,1)}, bf16[128,512]{1,0:T(8,128)(2,1)}) custom-call(bf16[640,1024]{1,0:T(8,128)(2,1)S(1)} %get-tuple-element.56.ds_ref, bf16[384,1024]{1,0:T(8,128)(2,1)S(1)} %get-tuple-element.57.w_ref, bf16[1024,640]{1,0:T(8,128)(2,1)S(1)} %shard_map.93.q2_ref, ...), custom_call_target="tpu_custom_call" | custom-call | flops 1140850688 | bytes 2621440 | tf_op jit(solution)/shard_map/own_gradients/pallas_call | solution.py:437
  34.1 1.9 %collective-permute-done.15.refs_2_ = bf16[32,640]{1,0:T(8,128)(2,1)S(1)} collective-permute-done((bf16[32,640]{1,0:T(8,128)(2,1)S(1)}, bf16[32,640]{1,0:T(8,128)(2,1)S(1)}, u32[]{:S(2)}, u32[]{:S(2)}) %collective-permute-start.15) | collective-permute-done | bytes 40992 | tf_op jit(solution)/shard_map/ppermute | solution.py:31
  36.0 1.3 %collective-permute-start.16 = (bf16[32,640]{1,0:T(8,128)(2,1)S(1)}, bf16[32,640]{1,0:T(8,128)(2,1)S(1)}, u32[]{:S(2)}, u32[]{:S(2)}) collective-permute-start(bf16[32,640]{1,0:T(8,128)(2,1)S(1)} %sum_four.1), channel_id=1, source_target_pairs={{0,16},{4,20},{8,24},{12,28},{16,0},{20,4},{24,8},{28,12},{1,17},{... | collective-permute-start | bytes 122888 | tf_op jit(solution)/shard_map/ppermute | solution.py:31
  37.4 1.1 %collective-permute-start.10 = (bf16[32,640]{1,0:T(8,128)(2,1)S(1)}, bf16[32,640]{1,0:T(8,128)(2,1)S(1)}, u32[]{:S(2)}, u32[]{:S(2)}) collective-permute-start(bf16[32,640]{1,0:T(8,128)(2,1)S(1)} %get-tuple-element.65), channel_id=1, source_target_pairs={{0,3},{1,0},{2,1},{3,2},{4,7},{5,4},{6,5},{7,6},{8,11},{9,8},{10,9... | collective-permute-start | bytes 122888 | tf_op jit(solution)/shard_map/ppermute | solution.py:31
  38.5 1.8 %collective-permute-start.12 = (bf16[32,640]{1,0:T(8,128)(2,1)S(1)}, bf16[32,640]{1,0:T(8,128)(2,1)S(1)}, u32[]{:S(2)}, u32[]{:S(2)}) collective-permute-start(bf16[32,640]{1,0:T(8,128)(2,1)S(1)} %get-tuple-element.67), channel_id=1, source_target_pairs={{0,1},{1,2},{2,3},{3,0},{4,5},{5,6},{6,7},{7,4},{8,9},{9,10},{10,1... | collective-permute-start | bytes 122888 | tf_op jit(solution)/shard_map/ppermute | solution.py:31
  40.2 1.6 %collective-permute-done.10.refs_0_ = bf16[32,640]{1,0:T(8,128)(2,1)S(1)} collective-permute-done((bf16[32,640]{1,0:T(8,128)(2,1)S(1)}, bf16[32,640]{1,0:T(8,128)(2,1)S(1)}, u32[]{:S(2)}, u32[]{:S(2)}) %collective-permute-start.10) | collective-permute-done | bytes 40992 | tf_op jit(solution)/shard_map/ppermute | solution.py:31
  41.9 1.5 %collective-permute-done.11.refs_1_ = bf16[32,640]{1,0:T(8,128)(2,1)S(1)} collective-permute-done((bf16[32,640]{1,0:T(8,128)(2,1)S(1)}, bf16[32,640]{1,0:T(8,128)(2,1)S(1)}, u32[]{:S(2)}, u32[]{:S(2)}) %collective-permute-start.11) | collective-permute-done | bytes 40992 | tf_op jit(solution)/shard_map/ppermute | solution.py:31
  43.4 0.9 %collective-permute-done.12.refs_2_ = bf16[32,640]{1,0:T(8,128)(2,1)S(1)} collective-permute-done((bf16[32,640]{1,0:T(8,128)(2,1)S(1)}, bf16[32,640]{1,0:T(8,128)(2,1)S(1)}, u32[]{:S(2)}, u32[]{:S(2)}) %collective-permute-start.12) | collective-permute-done | bytes 40992 | tf_op jit(solution)/shard_map/ppermute | solution.py:31
  (34 shorter events, 5.0 us)
Async XLA Ops:
  1.5 8.5 %collective-permute-start.2 = (bf16[32,640]{1,0:T(8,128)(2,1)S(1)}, bf16[32,640]{1,0:T(8,128)(2,1)S(1)}, u32[]{:S(2)}, u32[]{:S(2)}) collective-permute-start(bf16[32,640]{1,0:T(8,128)(2,1)S(1)} %pad_maximum_fusion), channel_id=1, source_target_pairs={{0,3},{1,0},{2,1},{3,2},{4,7},{5,4},{6,5},{7,6},{8,11},{9,8},{10,9... | collective-permute-start | bytes 122888 | tf_op jit(solution)/shard_map/ppermute | solution.py:31
  6.6 4.9 %collective-permute-start.1 = (bf16[32,640]{1,0:T(8,128)(2,1)S(1)}, bf16[32,640]{1,0:T(8,128)(2,1)S(1)}, u32[]{:S(2)}, u32[]{:S(2)}) collective-permute-start(bf16[32,640]{1,0:T(8,128)(2,1)S(1)} %pad_maximum_fusion), channel_id=1, source_target_pairs={{0,2},{1,3},{2,0},{3,1},{4,6},{5,7},{6,4},{7,5},{8,10},{9,11},{10,... | collective-permute-start | bytes 122888 | tf_op jit(solution)/shard_map/ppermute | solution.py:31
  6.6 5.8 %collective-permute-start = (bf16[32,640]{1,0:T(8,128)(2,1)S(1)}, bf16[32,640]{1,0:T(8,128)(2,1)S(1)}, u32[]{:S(2)}, u32[]{:S(2)}) collective-permute-start(bf16[32,640]{1,0:T(8,128)(2,1)S(1)} %pad_maximum_fusion), channel_id=1, source_target_pairs={{0,1},{1,2},{2,3},{3,0},{4,5},{5,6},{6,7},{7,4},{8,9},{9,10},{10,1... | collective-permute-start | bytes 122888 | tf_op jit(solution)/shard_map/ppermute | solution.py:31
  7.6 1.2 %copy-start = (bf16[128,4096]{1,0:T(8,128)(2,1)S(1)}, bf16[128,4096]{1,0:T(8,128)(2,1)}, u32[]{:S(2)}) copy-start(bf16[128,4096]{1,0:T(8,128)(2,1)} %x_ref.2) | copy-start | bytes 3145732
  8.8 0.9 %copy-start.2 = (bf16[128,512]{1,0:T(8,128)(2,1)S(1)}, bf16[128,512]{1,0:T(8,128)(2,1)}, u32[]{:S(2)}) copy-start(bf16[128,512]{1,0:T(8,128)(2,1)} %refs_0_.1) | copy-start | bytes 393220
  9.7 5.8 %copy-start.1 = (bf16[128,4096]{1,0:T(8,128)(2,1)S(1)}, bf16[128,4096]{1,0:T(8,128)(2,1)}, u32[]{:S(2)}) copy-start(bf16[128,4096]{1,0:T(8,128)(2,1)} %x_ref.3) | copy-start | bytes 3145732
  10.0 8.8 %copy-start.3 = (s32[1,5]{1,0:T(1,128)S(1)}, s32[1,5]{1,0:T(1,128)}, u32[]{:S(2)}) copy-start(s32[1,5]{1,0:T(1,128)} %pattern_ref.5) | copy-start | bytes 64
  12.4 6.4 %collective-permute-start.3 = (bf16[128,640]{1,0:T(8,128)(2,1)S(1)}, bf16[128,640]{1,0:T(8,128)(2,1)S(1)}, u32[]{:S(2)}, u32[]{:S(2)}) collective-permute-start(bf16[128,640]{1,0:T(8,128)(2,1)S(1)} %constant_dynamic-update-slice_fusion.refs_1_.refs_6_), channel_id=1, source_target_pairs={{0,8},{4,12},{8,16},{12,20},{16,24},{20,28},{24,0},{28,4},{1,9},{5... | collective-permute-start | bytes 491528 | tf_op jit(solution)/shard_map/ppermute | solution.py:31
  14.0 7.4 %collective-permute-start.4 = (bf16[128,640]{1,0:T(8,128)(2,1)S(1)}, bf16[128,640]{1,0:T(8,128)(2,1)S(1)}, u32[]{:S(2)}, u32[]{:S(2)}) collective-permute-start(bf16[128,640]{1,0:T(8,128)(2,1)S(1)} %constant_dynamic-update-slice_fusion.refs_1_.refs_6_), channel_id=1, source_target_pairs={{0,16},{4,20},{8,24},{12,28},{16,0},{20,4},{24,8},{28,12},{1,17},{... | collective-permute-start | bytes 491528 | tf_op jit(solution)/shard_map/ppermute | solution.py:31
  15.7 5.7 %collective-permute-start.5 = (bf16[128,640]{1,0:T(8,128)(2,1)S(1)}, bf16[128,640]{1,0:T(8,128)(2,1)S(1)}, u32[]{:S(2)}, u32[]{:S(2)}) collective-permute-start(bf16[128,640]{1,0:T(8,128)(2,1)S(1)} %constant_dynamic-update-slice_fusion.refs_1_.refs_6_), channel_id=1, source_target_pairs={{0,4},{4,0},{8,12},{12,8},{16,20},{20,16},{24,28},{28,24},{1,5},{5... | collective-permute-start | bytes 491528 | tf_op jit(solution)/shard_map/ppermute | solution.py:36
  18.8 2.6 %collective-permute-start.6 = (bf16[128,640]{1,0:T(8,128)(2,1)S(1)}, bf16[128,640]{1,0:T(8,128)(2,1)S(1)}, u32[]{:S(2)}, u32[]{:S(2)}) collective-permute-start(bf16[128,640]{1,0:T(8,128)(2,1)S(1)} %collective-permute-done.3.refs_0_.refs_7_), channel_id=1, source_target_pairs={{0,4},{4,0},{8,12},{12,8},{16,20},{20,16},{24,28},{28,24},{1,5},{5... | collective-permute-start | bytes 491528 | tf_op jit(solution)/shard_map/ppermute | solution.py:36
  21.4 1.6 %collective-permute-start.7 = (bf16[128,640]{1,0:T(8,128)(2,1)S(1)}, bf16[128,640]{1,0:T(8,128)(2,1)S(1)}, u32[]{:S(2)}, u32[]{:S(2)}) collective-permute-start(bf16[128,640]{1,0:T(8,128)(2,1)S(1)} %collective-permute-done.4.refs_0_.refs_8_), channel_id=1, source_target_pairs={{0,4},{4,0},{8,12},{12,8},{16,20},{20,16},{24,28},{28,24},{1,5},{5... | collective-permute-start | bytes 491528 | tf_op jit(solution)/shard_map/ppermute | solution.py:36
  25.7 1.8 %collective-permute-start.8 = (bf16[256,640]{1,0:T(8,128)(2,1)S(1)}, bf16[256,640]{1,0:T(8,128)(2,1)S(1)}, u32[]{:S(2)}, u32[]{:S(2)}) collective-permute-start(bf16[256,640]{1,0:T(8,128)(2,1)S(1)} %get-tuple-element.59), channel_id=1, source_target_pairs={{0,4},{4,0},{8,12},{12,8},{16,20},{20,16},{24,28},{28,24},{1,5},{5... | collective-permute-start | bytes 983048 | tf_op jit(solution)/shard_map/ppermute | solution.py:36
  27.6 9.8 %collective-permute-start.9 = (bf16[128,640]{1,0:T(8,128)(2,1)S(1)}, bf16[128,640]{1,0:T(8,128)(2,1)S(1)}, u32[]{:S(2)}, u32[]{:S(2)}) collective-permute-start(bf16[128,640]{1,0:T(8,128)(2,1)S(1)} %get-tuple-element.63), channel_id=1, source_target_pairs={{0,24},{4,28},{8,0},{12,4},{16,8},{20,12},{24,16},{28,20},{1,25},{... | collective-permute-start | bytes 491528 | tf_op jit(solution)/shard_map/ppermute | solution.py:31
  28.6 5.4 %collective-permute-start.13 = (bf16[32,640]{1,0:T(8,128)(2,1)S(1)}, bf16[32,640]{1,0:T(8,128)(2,1)S(1)}, u32[]{:S(2)}, u32[]{:S(2)}) collective-permute-start(bf16[32,640]{1,0:T(8,128)(2,1)S(1)} %get-tuple-element.69), channel_id=1, source_target_pairs={{0,3},{1,0},{2,1},{3,2},{4,7},{5,4},{6,5},{7,6},{8,11},{9,8},{10,9... | collective-permute-start | bytes 122888 | tf_op jit(solution)/shard_map/ppermute | solution.py:31
  29.2 4.9 %collective-permute-start.14 = (bf16[32,640]{1,0:T(8,128)(2,1)S(1)}, bf16[32,640]{1,0:T(8,128)(2,1)S(1)}, u32[]{:S(2)}, u32[]{:S(2)}) collective-permute-start(bf16[32,640]{1,0:T(8,128)(2,1)S(1)} %get-tuple-element.70), channel_id=1, source_target_pairs={{0,2},{1,3},{2,0},{3,1},{4,6},{5,7},{6,4},{7,5},{8,10},{9,11},{10,... | collective-permute-start | bytes 122888 | tf_op jit(solution)/shard_map/ppermute | solution.py:31
  30.2 5.8 %collective-permute-start.15 = (bf16[32,640]{1,0:T(8,128)(2,1)S(1)}, bf16[32,640]{1,0:T(8,128)(2,1)S(1)}, u32[]{:S(2)}, u32[]{:S(2)}) collective-permute-start(bf16[32,640]{1,0:T(8,128)(2,1)S(1)} %get-tuple-element.71), channel_id=1, source_target_pairs={{0,1},{1,2},{2,3},{3,0},{4,5},{5,6},{6,7},{7,4},{8,9},{9,10},{10,1... | collective-permute-start | bytes 122888 | tf_op jit(solution)/shard_map/ppermute | solution.py:31
  36.0 4.2 %collective-permute-start.16 = (bf16[32,640]{1,0:T(8,128)(2,1)S(1)}, bf16[32,640]{1,0:T(8,128)(2,1)S(1)}, u32[]{:S(2)}, u32[]{:S(2)}) collective-permute-start(bf16[32,640]{1,0:T(8,128)(2,1)S(1)} %sum_four.1), channel_id=1, source_target_pairs={{0,16},{4,20},{8,24},{12,28},{16,0},{20,4},{24,8},{28,12},{1,17},{... | collective-permute-start | bytes 122888 | tf_op jit(solution)/shard_map/ppermute | solution.py:31
  37.4 4.5 %collective-permute-start.10 = (bf16[32,640]{1,0:T(8,128)(2,1)S(1)}, bf16[32,640]{1,0:T(8,128)(2,1)S(1)}, u32[]{:S(2)}, u32[]{:S(2)}) collective-permute-start(bf16[32,640]{1,0:T(8,128)(2,1)S(1)} %get-tuple-element.65), channel_id=1, source_target_pairs={{0,3},{1,0},{2,1},{3,2},{4,7},{5,4},{6,5},{7,6},{8,11},{9,8},{10,9... | collective-permute-start | bytes 122888 | tf_op jit(solution)/shard_map/ppermute | solution.py:31
  38.5 4.9 %collective-permute-start.11 = (bf16[32,640]{1,0:T(8,128)(2,1)S(1)}, bf16[32,640]{1,0:T(8,128)(2,1)S(1)}, u32[]{:S(2)}, u32[]{:S(2)}) collective-permute-start(bf16[32,640]{1,0:T(8,128)(2,1)S(1)} %get-tuple-element.66), channel_id=1, source_target_pairs={{0,2},{1,3},{2,0},{3,1},{4,6},{5,7},{6,4},{7,5},{8,10},{9,11},{10,... | collective-permute-start | bytes 122888 | tf_op jit(solution)/shard_map/ppermute | solution.py:31
  38.5 5.8 %collective-permute-start.12 = (bf16[32,640]{1,0:T(8,128)(2,1)S(1)}, bf16[32,640]{1,0:T(8,128)(2,1)S(1)}, u32[]{:S(2)}, u32[]{:S(2)}) collective-permute-start(bf16[32,640]{1,0:T(8,128)(2,1)S(1)} %get-tuple-element.67), channel_id=1, source_target_pairs={{0,1},{1,2},{2,3},{3,0},{4,5},{5,6},{6,7},{7,4},{8,9},{9,10},{10,1... | collective-permute-start | bytes 122888 | tf_op jit(solution)/shard_map/ppermute | solution.py:31

commit v2 on v1

--- a/solution.py
+++ b/solution.py
@@ -237,9 +237,23 @@
     grad_ref[:, latent:] = turned
 
 
-def own_kernel(dims, ds_ref, w_ref, q2_ref, u2_ref, keys_ref, *refs):
-    own, pairs, tokens, latent, rope = dims
-    *met_refs, grad_ref, dq_ref, dr_ref, dq_scr, dr_scr, sems = refs
+def own_kernel(dims, ds_ref, w_ref, q2_ref, u2_ref, *refs):
+    own, tokens, latent = dims
+    *met_refs, grad_ref = refs
+    rows = slice(own * tokens, (own + 1) * tokens)
+    main, turned = key_gradient(
+        ds_ref[rows, :], w_ref[rows, :], q2_ref[...], u2_ref[...], latent
+    )
+    start = jnp.zeros(grad_ref.shape, F32)
+    for ref in met_refs:
+        is_odd = lax.rem(lax.axis_index("blk"), 2) == 1
+        start = jnp.where(is_odd, start, ref[:tokens, :].astype(F32))
+    grad_ref[:, :latent] = start[:, :latent] + main
+    grad_ref[:, latent:] = start[:, latent:] + turned
+
+
+def query_kernel(dims, ds_ref, keys_ref, dq_ref, dr_ref, dq_scr, dr_scr, sems):
+    pairs, tokens, latent, rope = dims
     tn = (((0,), (0,)), ((), ()))
     lane = lax.broadcasted_iota(jnp.int32, (tokens, 2 * rope), 1)
     copies = []
@@ -257,16 +271,6 @@
         copies[-1].start()
     copies.append(pltpu.make_async_copy(dr_scr, dr_ref, sems.at[pairs]))
     copies[-1].start()
-    rows = slice(own * tokens, (own + 1) * tokens)
-    main, turned = key_gradient(
-        ds_ref[rows, :], w_ref[rows, :], q2_ref[...], u2_ref[...], latent
-    )
-    start = jnp.zeros(grad_ref.shape, F32)
-    for ref in met_refs:
-        is_odd = lax.rem(lax.axis_index("blk"), 2) == 1
-        start = jnp.where(is_odd, start, ref[:tokens, :].astype(F32))
-    grad_ref[:, :latent] = start[:, :latent] + main
-    grad_ref[:, latent:] = start[:, latent:] + turned
     for copy in copies:
         copy.wait()
 
@@ -308,7 +312,7 @@
     q2 = staged(wide, query_latent, query_rotary)
     own = jnp.concatenate([latent, key_rotary, key_rotary], axis=1)
     gathered = [own] + [rotated(own, "inner", k) for k in range(1, inner)]
-    gathered, q2 = lax.optimization_barrier((gathered, q2))
+    gathered = lax.optimization_barrier(gathered)
     near = jnp.concatenate(gathered, axis=0)
     u2 = staged(width, upstream)
     if paired:
@@ -318,7 +322,7 @@
         two = rotated(near, "blk", 2)
         four = rotated(near, "blk", 4)
         near_met = swapped(near)
-        two, u2 = lax.optimization_barrier((two, u2))
+        two, q2, u2 = lax.optimization_barrier((two, q2, u2))
         two_met = swapped(two)
         sources = [(2,), (1,), (0,), (4, 3), (5, 4)]
     else:
@@ -434,12 +438,23 @@
         handed = []
         shards_back = []
 
-    own_grad, query_cotangent, rotary_cotangent = pl.pallas_call(
-        functools.partial(own_kernel, (kept - 1, pairs, tokens, width, rope)),
-        in_specs=[vmem] * (5 + len(handed)),
-        out_specs=[vmem, hbm, hbm],
+    own_grad = pl.pallas_call(
+        functools.partial(own_kernel, (kept - 1, tokens, width)),
+        out_shape=jax.ShapeDtypeStruct((tokens, wide), F32),
+        cost_estimate=pl.CostEstimate(
+            flops=2 * rows * tokens * (wide + width),
+            bytes_accessed=2 * rows * wide,
+            transcendentals=0,
+        ),
+        compiler_params=params,
+        name="own_gradients",
+    )(ds, weights, *queries, *handed)
+
+    query_cotangent, rotary_cotangent = pl.pallas_call(
+        functools.partial(query_kernel, (pairs, tokens, width, rope)),
+        in_specs=[vmem] * 2,
+        out_specs=[hbm] * 2,
         out_shape=[
-            jax.ShapeDtypeStruct((tokens, wide), F32),
             jax.ShapeDtypeStruct(query_latent.shape, BF16),
             jax.ShapeDtypeStruct(query_rotary.shape, BF16),
         ],
@@ -449,13 +464,13 @@
             pltpu.SemaphoreType.DMA((pairs + 1,)),
         ],
         cost_estimate=pl.CostEstimate(
-            flops=2 * rows * (tokens * (wide + width) + depth * wide),
+            flops=2 * rows * depth * wide,
             bytes_accessed=2 * rows * (wide + depth),
             transcendentals=0,
         ),
         compiler_params=params,
-        name="own_gradients",
-    )(ds, weights, *queries, keys, *handed)
+        name="query_cotangents",
+    )(ds, keys)
 
     parts = pl.pallas_call(
         functools.partial(total_kernel, len(back)),

time: 45.2 us -> 45.2 us (level)
  waiting for transfers between devices: 12.8 us -> 12.1 us
    ppermute x13, waiting for transfers between devices: 12.4 us -> 11.7 us  [rotated(): lax.ppermute(value, axis, [(s, (s + steps) % count) for s in range(count)])]
    pallas_call x1 -> x2, Pallas kernels: 2.26 us -> 2.58 us  [the longest x1 2.07 us: per_device(): pl.pallas_call(functools.partial(query_kernel, (pairs, tokens, width, rop...]
  transfers between devices with their start and end apart: 17 -> 17, of which waited for: 10 -> 11; matrix products, arithmetic and copies ran while one was open for 0% -> 0% of each run, Pallas kernels for 15% -> 16%
where the time goes in v2:
time: 45.2 us; the launch traced here: 45 us
  starting transfers between devices  18.4 us (41%)
  waiting for transfers between devices  12.1 us (27%)
  Pallas kernels  10.6 us (23%)
  local copies, waits for them, and re-layouts  2.24 us (5%)
  other arithmetic  0.9 us (2%)
  between operations  0.78 us (2%)
    ppermute x13, starting transfers between devices, rotated(): lax.ppermute(value, axis, [(s, (s + steps) % count) for s in range(count)])  17.7 us
    ppermute x13, waiting for transfers between devices, rotated(): lax.ppermute(value, axis, [(s, (s + steps) % count) for s in range(count)])  11.7 us
    pallas_call x2, Pallas kernels, early_scores(): pl.pallas_call(functools.partial(early_kernel, (pairs, tokens, shard, wid...  3.2 us
    pallas_call x1, Pallas kernels, per_device(): pl.pallas_call(functools.partial(scores_kernel, (nd, kept, pairs, tokens,...  2.63 us
    unnamed x11, local copies, waits for them, and re-layouts  2.23 us
    pallas_call x1, Pallas kernels, per_device(): pl.pallas_call(functools.partial(query_kernel, (pairs, tokens, width, rop...  2.07 us
    concatenate x1, other arithmetic, per_device(): own = jnp.concatenate([latent, key_rotary, key_rotary], axis=1)  0.9 us
  transfers between devices with their start and end apart: 17, of which 11 were waited for; matrix products, arithmetic and copies ran while one was open for 0% of the time, Pallas kernels for 16%

profile of v2, /device:TPU:0, one launch (start us, length us, event | category | flops | bytes accessed | tf_op | source)
XLA Modules:
  0.0 45.0 jit_solution(6231029616849861809)
XLA Ops:
  0.6 0.9 %pad_maximum_fusion = bf16[32,640]{1,0:T(8,128)(2,1)S(1)} fusion(bf16[32,64]{1,0:T(8,128)(2,1)} %param.10, bf16[32,512]{1,0:T(8,128)(2,1)} %param.9), kind=kLoop, calls=%fused_computation | loop fusion | flops 122880 | bytes 77824 | tf_op jit(solution)/shard_map/concatenate | solution.py:313
  1.5 5.1 %collective-permute-start.2 = (bf16[32,640]{1,0:T(8,128)(2,1)S(1)}, bf16[32,640]{1,0:T(8,128)(2,1)S(1)}, u32[]{:S(2)}, u32[]{:S(2)}) collective-permute-start(bf16[32,640]{1,0:T(8,128)(2,1)S(1)} %pad_maximum_fusion), channel_id=1, source_target_pairs={{0,3},{1,0},{2,1},{3,2},{4,7},{5,4},{6,5},{7,6},{8,11},{9,8},{10,9... | collective-permute-start | bytes 122888 | tf_op jit(solution)/shard_map/ppermute | solution.py:31
  6.6 1.0 %collective-permute-start = (bf16[32,640]{1,0:T(8,128)(2,1)S(1)}, bf16[32,640]{1,0:T(8,128)(2,1)S(1)}, u32[]{:S(2)}, u32[]{:S(2)}) collective-permute-start(bf16[32,640]{1,0:T(8,128)(2,1)S(1)} %pad_maximum_fusion), channel_id=1, source_target_pairs={{0,1},{1,2},{2,3},{3,0},{4,5},{5,6},{6,7},{7,4},{8,9},{9,10},{10,1... | collective-permute-start | bytes 122888 | tf_op jit(solution)/shard_map/ppermute | solution.py:31
  7.6 0.7 %collective-permute-done.2 = bf16[32,640]{1,0:T(8,128)(2,1)S(1)} collective-permute-done((bf16[32,640]{1,0:T(8,128)(2,1)S(1)}, bf16[32,640]{1,0:T(8,128)(2,1)S(1)}, u32[]{:S(2)}, u32[]{:S(2)}) %collective-permute-start.2) | collective-permute-done | bytes 40992 | tf_op jit(solution)/shard_map/ppermute | solution.py:31
  8.3 3.2 %collective-permute-done.1 = bf16[32,640]{1,0:T(8,128)(2,1)S(1)} collective-permute-done((bf16[32,640]{1,0:T(8,128)(2,1)S(1)}, bf16[32,640]{1,0:T(8,128)(2,1)S(1)}, u32[]{:S(2)}, u32[]{:S(2)}) %collective-permute-start.1) | collective-permute-done | bytes 40992 | tf_op jit(solution)/shard_map/ppermute | solution.py:31
  11.5 0.9 %collective-permute-done = bf16[32,640]{1,0:T(8,128)(2,1)S(1)} collective-permute-done((bf16[32,640]{1,0:T(8,128)(2,1)S(1)}, bf16[32,640]{1,0:T(8,128)(2,1)S(1)}, u32[]{:S(2)}, u32[]{:S(2)}) %collective-permute-start) | collective-permute-done | bytes 40992 | tf_op jit(solution)/shard_map/ppermute | solution.py:31
  12.5 1.5 %collective-permute-start.3 = (bf16[128,640]{1,0:T(8,128)(2,1)S(1)}, bf16[128,640]{1,0:T(8,128)(2,1)S(1)}, u32[]{:S(2)}, u32[]{:S(2)}) collective-permute-start(bf16[128,640]{1,0:T(8,128)(2,1)S(1)} %constant_dynamic-update-slice_fusion.refs_1_.refs_6_), channel_id=1, source_target_pairs={{0,8},{4,12},{8,16},{12,20},{16,24},{20,28},{24,0},{28,4},{1,9},{5... | collective-permute-start | bytes 491528 | tf_op jit(solution)/shard_map/ppermute | solution.py:31
  14.0 1.5 %collective-permute-start.4 = (bf16[128,640]{1,0:T(8,128)(2,1)S(1)}, bf16[128,640]{1,0:T(8,128)(2,1)S(1)}, u32[]{:S(2)}, u32[]{:S(2)}) collective-permute-start(bf16[128,640]{1,0:T(8,128)(2,1)S(1)} %constant_dynamic-update-slice_fusion.refs_1_.refs_6_), channel_id=1, source_target_pairs={{0,16},{4,20},{8,24},{12,28},{16,0},{20,4},{24,8},{28,12},{1,17},{... | collective-permute-start | bytes 491528 | tf_op jit(solution)/shard_map/ppermute | solution.py:31
  15.5 1.2 %copy-done = bf16[128,4096]{1,0:T(8,128)(2,1)S(1)} copy-done((bf16[128,4096]{1,0:T(8,128)(2,1)S(1)}, bf16[128,4096]{1,0:T(8,128)(2,1)}, u32[]{:S(2)}) %copy-start) | copy-done | bytes 1048600
  17.0 1.0 %copy-done.1 = bf16[128,4096]{1,0:T(8,128)(2,1)S(1)} copy-done((bf16[128,4096]{1,0:T(8,128)(2,1)S(1)}, bf16[128,4096]{1,0:T(8,128)(2,1)}, u32[]{:S(2)}) %copy-start.1) | copy-done | bytes 1048600
  18.9 1.6 %shard_map.95 = (f32[256,1024]{1,0:T(8,128)S(1)}, f32[256,1024]{1,0:T(8,128)S(1)}, f32[8,1024]{1,0:T(8,128)S(1)}) custom-call(s32[1,5]{1,0:T(1,128)S(1)} %copy-done.3, bf16[1024,640]{1,0:T(8,128)(2,1)S(1)} %shard_map.93.q2_ref, bf16[1024,512]{1,0:T(8,128)(2,1)S(1)} %shard_map.94.u2_ref, bf16[128,640]{1,0:T(8,128)(2,1)S(1)} %collective-permute-done.3.refs_0_.refs_7_, ...), custom_call_target="tpu_custom_call" | custom-call | flops 603979776 | bytes 2097152 | tf_op jit(solution)/shard_map/pallas_call | solution.py:339
  20.5 1.0 %collective-permute-done.4.refs_0_.refs_8_ = bf16[128,640]{1,0:T(8,128)(2,1)S(1)} collective-permute-done((bf16[128,640]{1,0:T(8,128)(2,1)S(1)}, bf16[128,640]{1,0:T(8,128)(2,1)S(1)}, u32[]{:S(2)}, u32[]{:S(2)}) %collective-permute-start.4) | collective-permute-done | bytes 163872 | tf_op jit(solution)/shard_map/ppermute | solution.py:31
  21.5 1.6 %shard_map.96 = (f32[256,1024]{1,0:T(8,128)S(1)}, f32[256,1024]{1,0:T(8,128)S(1)}, f32[8,1024]{1,0:T(8,128)S(1)}) custom-call(s32[1,5]{1,0:T(1,128)S(1)} %copy-done.3, bf16[1024,640]{1,0:T(8,128)(2,1)S(1)} %shard_map.93.q2_ref, bf16[1024,512]{1,0:T(8,128)(2,1)S(1)} %shard_map.94.u2_ref, bf16[128,640]{1,0:T(8,128)(2,1)S(1)} %collective-permute-done.4.refs_0_.refs_8_, ...), custom_call_target="tpu_custom_call" | custom-call | flops 603979776 | bytes 2097152 | tf_op jit(solution)/shard_map/pallas_call | solution.py:339
  23.1 2.6 %scores.1 = (bf16[640,1024]{1,0:T(8,128)(2,1)S(1)}, bf16[384,1024]{1,0:T(8,128)(2,1)S(1)}, bf16[640,640]{1,0:T(8,128)(2,1)S(1)}, bf16[256,640]{1,0:T(8,128)(2,1)S(1)}) custom-call(s32[1,5]{1,0:T(1,128)S(1)} %copy-done.3, bf16[1024,640]{1,0:T(8,128)(2,1)S(1)} %shard_map.93.q2_ref, bf16[1024,512]{1,0:T(8,128)(2,1)S(1)} %shard_map.94.u2_ref, ...), custom_call_target="tpu_custom_call" | custom-call | flops 905969664 | bytes 5242880 | tf_op jit(solution)/shard_map/scores/pallas_call | solution.py:374
  26.3 0.8 %late_gradients.1.late_ref = f32[256,640]{1,0:T(8,128)S(1)} custom-call(bf16[640,1024]{1,0:T(8,128)(2,1)S(1)} %get-tuple-element.55.ds_ref, bf16[384,1024]{1,0:T(8,128)(2,1)S(1)} %get-tuple-element.59.w_ref, bf16[1024,640]{1,0:T(8,128)(2,1)S(1)} %shard_map.93.q2_ref, bf16[1024,512]{1,0:T(8,128)(2,1)S(1)} %shard_map.94.u2_ref), custom_call_target="tpu_custom_call" | custom-call | flops 603979776 | bytes 2621440 | tf_op jit(solution)/shard_map/late_gradients/pallas_call | solution.py:406
  27.6 1.0 %collective-permute-start.9 = (bf16[128,640]{1,0:T(8,128)(2,1)S(1)}, bf16[128,640]{1,0:T(8,128)(2,1)S(1)}, u32[]{:S(2)}, u32[]{:S(2)}) collective-permute-start(bf16[128,640]{1,0:T(8,128)(2,1)S(1)} %get-tuple-element.61), channel_id=1, source_target_pairs={{0,24},{4,28},{8,0},{12,4},{16,8},{20,12},{24,16},{28,20},{1,25},{... | collective-permute-start | bytes 491528 | tf_op jit(solution)/shard_map/ppermute | solution.py:31
  29.7 2.0 %collective-permute-start.15 = (bf16[32,640]{1,0:T(8,128)(2,1)S(1)}, bf16[32,640]{1,0:T(8,128)(2,1)S(1)}, u32[]{:S(2)}, u32[]{:S(2)}) collective-permute-start(bf16[32,640]{1,0:T(8,128)(2,1)S(1)} %get-tuple-element.69), channel_id=1, source_target_pairs={{0,1},{1,2},{2,3},{3,0},{4,5},{5,6},{6,7},{7,4},{8,9},{9,10},{10,1... | collective-permute-start | bytes 122888 | tf_op jit(solution)/shard_map/ppermute | solution.py:31
  32.3 0.8 %collective-permute-done.13.refs_0_ = bf16[32,640]{1,0:T(8,128)(2,1)S(1)} collective-permute-done((bf16[32,640]{1,0:T(8,128)(2,1)S(1)}, bf16[32,640]{1,0:T(8,128)(2,1)S(1)}, u32[]{:S(2)}, u32[]{:S(2)}) %collective-permute-start.13) | collective-permute-done | bytes 40992 | tf_op jit(solution)/shard_map/ppermute | solution.py:31
  33.1 2.0 %collective-permute-done.14.refs_1_ = bf16[32,640]{1,0:T(8,128)(2,1)S(1)} collective-permute-done((bf16[32,640]{1,0:T(8,128)(2,1)S(1)}, bf16[32,640]{1,0:T(8,128)(2,1)S(1)}, u32[]{:S(2)}, u32[]{:S(2)}) %collective-permute-start.14) | collective-permute-done | bytes 40992 | tf_op jit(solution)/shard_map/ppermute | solution.py:31
  35.6 1.3 %collective-permute-start.16 = (bf16[32,640]{1,0:T(8,128)(2,1)S(1)}, bf16[32,640]{1,0:T(8,128)(2,1)S(1)}, u32[]{:S(2)}, u32[]{:S(2)}) collective-permute-start(bf16[32,640]{1,0:T(8,128)(2,1)S(1)} %sum_four.1), channel_id=1, source_target_pairs={{0,16},{4,20},{8,24},{12,28},{16,0},{20,4},{24,8},{28,12},{1,17},{... | collective-permute-start | bytes 122888 | tf_op jit(solution)/shard_map/ppermute | solution.py:31
  36.9 1.6 %collective-permute-start.10 = (bf16[32,640]{1,0:T(8,128)(2,1)S(1)}, bf16[32,640]{1,0:T(8,128)(2,1)S(1)}, u32[]{:S(2)}, u32[]{:S(2)}) collective-permute-start(bf16[32,640]{1,0:T(8,128)(2,1)S(1)} %get-tuple-element.63), channel_id=1, source_target_pairs={{0,3},{1,0},{2,1},{3,2},{4,7},{5,4},{6,5},{7,6},{8,11},{9,8},{10,9... | collective-permute-start | bytes 122888 | tf_op jit(solution)/shard_map/ppermute | solution.py:31
  38.5 1.5 %collective-permute-start.12 = (bf16[32,640]{1,0:T(8,128)(2,1)S(1)}, bf16[32,640]{1,0:T(8,128)(2,1)S(1)}, u32[]{:S(2)}, u32[]{:S(2)}) collective-permute-start(bf16[32,640]{1,0:T(8,128)(2,1)S(1)} %get-tuple-element.65), channel_id=1, source_target_pairs={{0,1},{1,2},{2,3},{3,0},{4,5},{5,6},{6,7},{7,4},{8,9},{9,10},{10,1... | collective-permute-start | bytes 122888 | tf_op jit(solution)/shard_map/ppermute | solution.py:31
  40.1 2.1 %query_cotangents.1 = (bf16[128,4096]{1,0:T(8,128)(2,1)}, bf16[128,512]{1,0:T(8,128)(2,1)}) custom-call(bf16[640,1024]{1,0:T(8,128)(2,1)S(1)} %get-tuple-element.55.ds_ref, bf16[640,640]{1,0:T(8,128)(2,1)S(1)} %get-tuple-element.56.keys_ref), custom_call_target="tpu_custom_call" | custom-call | flops 838860800 | bytes 2621440 | tf_op jit(solution)/shard_map/query_cotangents/pallas_call | solution.py:453
  42.2 1.6 %collective-permute-done.11.refs_1_ = bf16[32,640]{1,0:T(8,128)(2,1)S(1)} collective-permute-done((bf16[32,640]{1,0:T(8,128)(2,1)S(1)}, bf16[32,640]{1,0:T(8,128)(2,1)S(1)}, u32[]{:S(2)}, u32[]{:S(2)}) %collective-permute-start.11) | collective-permute-done | bytes 40992 | tf_op jit(solution)/shard_map/ppermute | solution.py:31
  (35 shorter events, 5.8 us)
Async XLA Ops:
  0.6 16.4 %copy-start.2 = (bf16[128,512]{1,0:T(8,128)(2,1)S(1)}, bf16[128,512]{1,0:T(8,128)(2,1)}, u32[]{:S(2)}) copy-start(bf16[128,512]{1,0:T(8,128)(2,1)} %refs_0_.1) | copy-start | bytes 393220
  1.5 6.8 %collective-permute-start.2 = (bf16[32,640]{1,0:T(8,128)(2,1)S(1)}, bf16[32,640]{1,0:T(8,128)(2,1)S(1)}, u32[]{:S(2)}, u32[]{:S(2)}) collective-permute-start(bf16[32,640]{1,0:T(8,128)(2,1)S(1)} %pad_maximum_fusion), channel_id=1, source_target_pairs={{0,3},{1,0},{2,1},{3,2},{4,7},{5,4},{6,5},{7,6},{8,11},{9,8},{10,9... | collective-permute-start | bytes 122888 | tf_op jit(solution)/shard_map/ppermute | solution.py:31
  6.6 4.9 %collective-permute-start.1 = (bf16[32,640]{1,0:T(8,128)(2,1)S(1)}, bf16[32,640]{1,0:T(8,128)(2,1)S(1)}, u32[]{:S(2)}, u32[]{:S(2)}) collective-permute-start(bf16[32,640]{1,0:T(8,128)(2,1)S(1)} %pad_maximum_fusion), channel_id=1, source_target_pairs={{0,2},{1,3},{2,0},{3,1},{4,6},{5,7},{6,4},{7,5},{8,10},{9,11},{10,... | collective-permute-start | bytes 122888 | tf_op jit(solution)/shard_map/ppermute | solution.py:31
  6.6 5.8 %collective-permute-start = (bf16[32,640]{1,0:T(8,128)(2,1)S(1)}, bf16[32,640]{1,0:T(8,128)(2,1)S(1)}, u32[]{:S(2)}, u32[]{:S(2)}) collective-permute-start(bf16[32,640]{1,0:T(8,128)(2,1)S(1)} %pad_maximum_fusion), channel_id=1, source_target_pairs={{0,1},{1,2},{2,3},{3,0},{4,5},{5,6},{6,7},{7,4},{8,9},{9,10},{10,1... | collective-permute-start | bytes 122888 | tf_op jit(solution)/shard_map/ppermute | solution.py:31
  12.5 6.4 %collective-permute-start.3 = (bf16[128,640]{1,0:T(8,128)(2,1)S(1)}, bf16[128,640]{1,0:T(8,128)(2,1)S(1)}, u32[]{:S(2)}, u32[]{:S(2)}) collective-permute-start(bf16[128,640]{1,0:T(8,128)(2,1)S(1)} %constant_dynamic-update-slice_fusion.refs_1_.refs_6_), channel_id=1, source_target_pairs={{0,8},{4,12},{8,16},{12,20},{16,24},{20,28},{24,0},{28,4},{1,9},{5... | collective-permute-start | bytes 491528 | tf_op jit(solution)/shard_map/ppermute | solution.py:31
  14.0 7.4 %collective-permute-start.4 = (bf16[128,640]{1,0:T(8,128)(2,1)S(1)}, bf16[128,640]{1,0:T(8,128)(2,1)S(1)}, u32[]{:S(2)}, u32[]{:S(2)}) collective-permute-start(bf16[128,640]{1,0:T(8,128)(2,1)S(1)} %constant_dynamic-update-slice_fusion.refs_1_.refs_6_), channel_id=1, source_target_pairs={{0,16},{4,20},{8,24},{12,28},{16,0},{20,4},{24,8},{28,12},{1,17},{... | collective-permute-start | bytes 491528 | tf_op jit(solution)/shard_map/ppermute | solution.py:31
  15.5 1.2 %copy-start = (bf16[128,4096]{1,0:T(8,128)(2,1)S(1)}, bf16[128,4096]{1,0:T(8,128)(2,1)}, u32[]{:S(2)}) copy-start(bf16[128,4096]{1,0:T(8,128)(2,1)} %x_ref.3) | copy-start | bytes 3145732
  16.8 1.2 %copy-start.1 = (bf16[128,4096]{1,0:T(8,128)(2,1)S(1)}, bf16[128,4096]{1,0:T(8,128)(2,1)}, u32[]{:S(2)}) copy-start(bf16[128,4096]{1,0:T(8,128)(2,1)} %x_ref.2) | copy-start | bytes 3145732
  18.0 0.9 %copy-start.3 = (s32[1,5]{1,0:T(1,128)S(1)}, s32[1,5]{1,0:T(1,128)}, u32[]{:S(2)}) copy-start(s32[1,5]{1,0:T(1,128)} %pattern_ref.5) | copy-start | bytes 64
  18.3 3.2 %collective-permute-start.5 = (bf16[128,640]{1,0:T(8,128)(2,1)S(1)}, bf16[128,640]{1,0:T(8,128)(2,1)S(1)}, u32[]{:S(2)}, u32[]{:S(2)}) collective-permute-start(bf16[128,640]{1,0:T(8,128)(2,1)S(1)} %constant_dynamic-update-slice_fusion.refs_1_.refs_6_), channel_id=1, source_target_pairs={{0,4},{4,0},{8,12},{12,8},{16,20},{20,16},{24,28},{28,24},{1,5},{5... | collective-permute-start | bytes 491528 | tf_op jit(solution)/shard_map/ppermute | solution.py:36
  18.8 2.6 %collective-permute-start.6 = (bf16[128,640]{1,0:T(8,128)(2,1)S(1)}, bf16[128,640]{1,0:T(8,128)(2,1)S(1)}, u32[]{:S(2)}, u32[]{:S(2)}) collective-permute-start(bf16[128,640]{1,0:T(8,128)(2,1)S(1)} %collective-permute-done.3.refs_0_.refs_7_), channel_id=1, source_target_pairs={{0,4},{4,0},{8,12},{12,8},{16,20},{20,16},{24,28},{28,24},{1,5},{5... | collective-permute-start | bytes 491528 | tf_op jit(solution)/shard_map/ppermute | solution.py:36
  21.4 1.6 %collective-permute-start.7 = (bf16[128,640]{1,0:T(8,128)(2,1)S(1)}, bf16[128,640]{1,0:T(8,128)(2,1)S(1)}, u32[]{:S(2)}, u32[]{:S(2)}) collective-permute-start(bf16[128,640]{1,0:T(8,128)(2,1)S(1)} %collective-permute-done.4.refs_0_.refs_8_), channel_id=1, source_target_pairs={{0,4},{4,0},{8,12},{12,8},{16,20},{20,16},{24,28},{28,24},{1,5},{5... | collective-permute-start | bytes 491528 | tf_op jit(solution)/shard_map/ppermute | solution.py:36
  25.7 1.8 %collective-permute-start.8 = (bf16[256,640]{1,0:T(8,128)(2,1)S(1)}, bf16[256,640]{1,0:T(8,128)(2,1)S(1)}, u32[]{:S(2)}, u32[]{:S(2)}) collective-permute-start(bf16[256,640]{1,0:T(8,128)(2,1)S(1)} %get-tuple-element.60), channel_id=1, source_target_pairs={{0,4},{4,0},{8,12},{12,8},{16,20},{20,16},{24,28},{28,24},{1,5},{5... | collective-permute-start | bytes 983048 | tf_op jit(solution)/shard_map/ppermute | solution.py:36
  27.6 9.2 %collective-permute-start.9 = (bf16[128,640]{1,0:T(8,128)(2,1)S(1)}, bf16[128,640]{1,0:T(8,128)(2,1)S(1)}, u32[]{:S(2)}, u32[]{:S(2)}) collective-permute-start(bf16[128,640]{1,0:T(8,128)(2,1)S(1)} %get-tuple-element.61), channel_id=1, source_target_pairs={{0,24},{4,28},{8,0},{12,4},{16,8},{20,12},{24,16},{28,20},{1,25},{... | collective-permute-start | bytes 491528 | tf_op jit(solution)/shard_map/ppermute | solution.py:31
  28.6 4.4 %collective-permute-start.13 = (bf16[32,640]{1,0:T(8,128)(2,1)S(1)}, bf16[32,640]{1,0:T(8,128)(2,1)S(1)}, u32[]{:S(2)}, u32[]{:S(2)}) collective-permute-start(bf16[32,640]{1,0:T(8,128)(2,1)S(1)} %get-tuple-element.67), channel_id=1, source_target_pairs={{0,3},{1,0},{2,1},{3,2},{4,7},{5,4},{6,5},{7,6},{8,11},{9,8},{10,9... | collective-permute-start | bytes 122888 | tf_op jit(solution)/shard_map/ppermute | solution.py:31
  29.3 5.8 %collective-permute-start.14 = (bf16[32,640]{1,0:T(8,128)(2,1)S(1)}, bf16[32,640]{1,0:T(8,128)(2,1)S(1)}, u32[]{:S(2)}, u32[]{:S(2)}) collective-permute-start(bf16[32,640]{1,0:T(8,128)(2,1)S(1)} %get-tuple-element.68), channel_id=1, source_target_pairs={{0,2},{1,3},{2,0},{3,1},{4,6},{5,7},{6,4},{7,5},{8,10},{9,11},{10,... | collective-permute-start | bytes 122888 | tf_op jit(solution)/shard_map/ppermute | solution.py:31
  29.7 5.8 %collective-permute-start.15 = (bf16[32,640]{1,0:T(8,128)(2,1)S(1)}, bf16[32,640]{1,0:T(8,128)(2,1)S(1)}, u32[]{:S(2)}, u32[]{:S(2)}) collective-permute-start(bf16[32,640]{1,0:T(8,128)(2,1)S(1)} %get-tuple-element.69), channel_id=1, source_target_pairs={{0,1},{1,2},{2,3},{3,0},{4,5},{5,6},{6,7},{7,4},{8,9},{9,10},{10,1... | collective-permute-start | bytes 122888 | tf_op jit(solution)/shard_map/ppermute | solution.py:31
  35.6 6.6 %collective-permute-start.16 = (bf16[32,640]{1,0:T(8,128)(2,1)S(1)}, bf16[32,640]{1,0:T(8,128)(2,1)S(1)}, u32[]{:S(2)}, u32[]{:S(2)}) collective-permute-start(bf16[32,640]{1,0:T(8,128)(2,1)S(1)} %sum_four.1), channel_id=1, source_target_pairs={{0,16},{4,20},{8,24},{12,28},{16,0},{20,4},{24,8},{28,12},{1,17},{... | collective-permute-start | bytes 122888 | tf_op jit(solution)/shard_map/ppermute | solution.py:31
  36.9 5.3 %collective-permute-start.10 = (bf16[32,640]{1,0:T(8,128)(2,1)S(1)}, bf16[32,640]{1,0:T(8,128)(2,1)S(1)}, u32[]{:S(2)}, u32[]{:S(2)}) collective-permute-start(bf16[32,640]{1,0:T(8,128)(2,1)S(1)} %get-tuple-element.63), channel_id=1, source_target_pairs={{0,3},{1,0},{2,1},{3,2},{4,7},{5,4},{6,5},{7,6},{8,11},{9,8},{10,9... | collective-permute-start | bytes 122888 | tf_op jit(solution)/shard_map/ppermute | solution.py:31
  38.5 5.2 %collective-permute-start.11 = (bf16[32,640]{1,0:T(8,128)(2,1)S(1)}, bf16[32,640]{1,0:T(8,128)(2,1)S(1)}, u32[]{:S(2)}, u32[]{:S(2)}) collective-permute-start(bf16[32,640]{1,0:T(8,128)(2,1)S(1)} %get-tuple-element.64), channel_id=1, source_target_pairs={{0,2},{1,3},{2,0},{3,1},{4,6},{5,7},{6,4},{7,5},{8,10},{9,11},{10,... | collective-permute-start | bytes 122888 | tf_op jit(solution)/shard_map/ppermute | solution.py:31
  38.5 5.8 %collective-permute-start.12 = (bf16[32,640]{1,0:T(8,128)(2,1)S(1)}, bf16[32,640]{1,0:T(8,128)(2,1)S(1)}, u32[]{:S(2)}, u32[]{:S(2)}) collective-permute-start(bf16[32,640]{1,0:T(8,128)(2,1)S(1)} %get-tuple-element.65), channel_id=1, source_target_pairs={{0,1},{1,2},{2,3},{3,0},{4,5},{5,6},{6,7},{7,4},{8,9},{9,10},{10,1... | collective-permute-start | bytes 122888 | tf_op jit(solution)/shard_map/ppermute | solution.py:31

commit v3 on v2

--- a/solution.py
+++ b/solution.py
@@ -172,9 +172,8 @@
 def scores_kernel(dims, groups, sources, entries, pattern_ref, q2_ref, u2_ref, *refs):
     nd, kept, pairs, tokens, latent, scale = dims
     early = [refs[3 * g : 3 * g + 3] for g in range(len(groups))]
-    ds_ref, kept_ref, keys, grad_ref, tail, s_scr, t_scr, w_scr = refs[-8:]
-    key_refs = refs[3 * len(groups) : -8]
-    place_keys(keys, key_refs, sources, tokens)
+    ds_ref, rows_ref, grad_ref, tail, s_scr, t_scr, w_scr = refs[-7:]
+    key_refs = refs[3 * len(groups) : -7]
     later = [d for d in range(nd) if not any(d in group for group in groups)]
     place_keys(tail, key_refs, [sources[d] for d in later], tokens)
     chosen = [pattern_ref[0, entries[d]] >= 0 for d in later]
@@ -207,7 +206,10 @@
         inverse = 1.0 / total
         correction = mixed * inverse
         factors = [f * inverse for f in shrink]
-        for d in range(nd):
+        rows_ref[0:1, lanes] = correction
+        for g, factor in enumerate(factors):
+            rows_ref[g + 1 : g + 2, lanes] = factor
+        for d in range(kept, nd):
             if d in later:
                 k = later.index(d)
                 e, dp, factor = s_scr[slot, block(k), :], t_scr[slot, block(k), :], inverse
@@ -215,34 +217,41 @@
                 g = [d in group for group in groups].index(True)
                 source = block(groups[g].index(d))
                 e, dp, factor = early[g][0][source, lanes], early[g][1][source, lanes], factors[g]
-            w = (e * factor).astype(BF16)
-            if d < kept:
-                kept_ref[block(d), lanes] = w
-            else:
-                w_scr[block(d - kept), lanes] = w
-            ds_ref[block(d), lanes] = (e * (factor * scale) * (dp - correction)).astype(BF16)
-    main, turned = key_gradient(
-        ds_ref[kept * tokens :, :], w_scr[...], q2_ref[...], u2_ref[...], latent
-    )
+            w_scr[block(d - kept), lanes] = (e * factor).astype(BF16)
+            ds_ref[block(d - kept), lanes] = (e * (factor * scale) * (dp - correction)).astype(BF16)
+    main, turned = key_gradient(ds_ref[...], w_scr[...], q2_ref[...], u2_ref[...], latent)
     grad_ref[:, :latent] = main.astype(BF16)
     grad_ref[:, latent:] = turned.astype(BF16)
 
 
-def gradient_kernel(dims, ds_ref, w_ref, q2_ref, u2_ref, grad_ref):
-    late, latent = dims
-    main, turned = key_gradient(
-        ds_ref[:late, :], w_ref[:late, :], q2_ref[...], u2_ref[...], latent
-    )
+def kept_gradient(dims, picks, rows_ref, early_refs, q2_ref, u2_ref, ds_ref, w_scr):
+    pairs, tokens, latent, scale = dims
+    for p in range(pairs):
+        lanes = slice(2 * p * tokens, 2 * (p + 1) * tokens)
+        correction = rows_ref[0:1, lanes]
+        for k, (g, place) in enumerate(picks):
+            factor = rows_ref[g + 1 : g + 2, lanes]
+            source = slice(place * tokens, (place + 1) * tokens)
+            rows = slice(k * tokens, (k + 1) * tokens)
+            e, dp = early_refs[2 * g][source, lanes], early_refs[2 * g + 1][source, lanes]
+            w_scr[rows, lanes] = (e * factor).astype(BF16)
+            ds_ref[rows, lanes] = (e * (factor * scale) * (dp - correction)).astype(BF16)
+    return key_gradient(ds_ref[...], w_scr[...], q2_ref[...], u2_ref[...], latent)
+
+
+def gradient_kernel(dims, picks, rows_ref, q2_ref, u2_ref, *refs):
+    *early_refs, grad_ref, ds_ref, w_scr = refs
+    latent = dims[2]
+    main, turned = kept_gradient(dims, picks, rows_ref, early_refs, q2_ref, u2_ref, ds_ref, w_scr)
     grad_ref[:, :latent] = main
     grad_ref[:, latent:] = turned
 
 
-def own_kernel(dims, ds_ref, w_ref, q2_ref, u2_ref, *refs):
-    own, tokens, latent = dims
-    *met_refs, grad_ref = refs
-    rows = slice(own * tokens, (own + 1) * tokens)
-    main, turned = key_gradient(
-        ds_ref[rows, :], w_ref[rows, :], q2_ref[...], u2_ref[...], latent
+def own_kernel(dims, picks, rows_ref, q2_ref, u2_ref, e_ref, p_ref, *refs):
+    *met_refs, grad_ref, ds_ref, w_scr = refs
+    tokens, latent = dims[1:3]
+    main, turned = kept_gradient(
+        dims, picks, rows_ref, (e_ref, p_ref), q2_ref, u2_ref, ds_ref, w_scr
     )
     start = jnp.zeros(grad_ref.shape, F32)
     for ref in met_refs:
@@ -252,8 +261,14 @@
     grad_ref[:, latent:] = start[:, latent:] + turned
 
 
-def query_kernel(dims, ds_ref, keys_ref, dq_ref, dr_ref, dq_scr, dr_scr, sems):
+def query_kernel(dims, sources, pieces, *refs):
     pairs, tokens, latent, rope = dims
+    dq_ref, dr_ref, dq_scr, dr_scr, ds_ref, keys_ref, sems = refs[-7:]
+    place_keys(keys_ref, refs[pieces:-7], sources, tokens)
+    at = 0
+    for ref in refs[:pieces]:
+        ds_ref[at : at + ref.shape[0], :] = ref[...]
+        at += ref.shape[0]
     tn = (((0,), (0,)), ((), ()))
     lane = lax.broadcasted_iota(jnp.int32, (tokens, 2 * rope), 1)
     copies = []
@@ -371,16 +386,15 @@
         key_arrays = [near] + [rotated(near, "blk", d) for d in spacing[1:]]
     queries = (q2, u2)
 
-    ds, weights, keys, grads = pl.pallas_call(
+    ds_sent, row_values, grads = pl.pallas_call(
         functools.partial(
             scores_kernel, (nd, kept, pairs, tokens, width, scale), groups, sources, entries
         ),
         in_specs=[smem] + [vmem] * (2 + len(early) + len(key_arrays)),
-        out_specs=[vmem] * 4,
+        out_specs=[vmem] * 3,
         out_shape=[
-            jax.ShapeDtypeStruct((depth, rows), BF16),
-            jax.ShapeDtypeStruct((kept * tokens, rows), BF16),
-            jax.ShapeDtypeStruct((depth, wide), BF16),
+            jax.ShapeDtypeStruct((sent * tokens, rows), BF16),
+            jax.ShapeDtypeStruct((8, rows), F32),
             jax.ShapeDtypeStruct((sent * tokens, wide), BF16),
         ],
         scratch_shapes=[
@@ -401,19 +415,27 @@
     part_shapes = [
         jax.ShapeDtypeStruct((shard, wide), F32 if k == 0 else BF16) for k in range(inner)
     ]
+    wide_dims = (pairs, tokens, width, scale)
+    exponents = [x for k, x in enumerate(early) if k % 3 < 2]
+    place_of = lambda d: [(g, group.index(d)) for g, group in enumerate(groups) if d in group][0]
     if paired:
         met = swapped(grads)
-        late = pl.pallas_call(
-            functools.partial(gradient_kernel, ((kept - 1) * tokens, width)),
-            out_shape=jax.ShapeDtypeStruct(((kept - 1) * tokens, wide), F32),
+        late_rows = (kept - 1) * tokens
+        late, ds_late = pl.pallas_call(
+            functools.partial(gradient_kernel, wide_dims, [place_of(d) for d in range(kept - 1)]),
+            out_shape=[
+                jax.ShapeDtypeStruct((late_rows, wide), F32),
+                jax.ShapeDtypeStruct((late_rows, rows), BF16),
+            ],
+            scratch_shapes=[pltpu.VMEM((late_rows, rows), BF16)],
             cost_estimate=pl.CostEstimate(
-                flops=2 * rows * (kept - 1) * tokens * (wide + width),
+                flops=2 * rows * late_rows * (wide + width),
                 bytes_accessed=4 * rows * wide,
                 transcendentals=0,
             ),
             compiler_params=params,
             name="late_gradients",
-        )(ds, weights, *queries)
+        )(row_values, *queries, *exponents)
         to_two, *four_parts = pl.pallas_call(
             merge_kernel,
             out_shape=[jax.ShapeDtypeStruct((tokens, wide), BF16)] + part_shapes,
@@ -430,17 +452,23 @@
         )(four_parts[0], *four_moved)
         shards_back = [rotated(four_shard, "blk", -4)]
         handed = [met]
+        ds_pieces = [ds_late]
     else:
         back = [
             rotated(grads[k * tokens : (k + 1) * tokens], "blk", -d)
             for k, d in enumerate(spacing[1:])
         ]
         handed = []
+        ds_pieces = []
         shards_back = []
 
-    own_grad = pl.pallas_call(
-        functools.partial(own_kernel, (kept - 1, tokens, width)),
-        out_shape=jax.ShapeDtypeStruct((tokens, wide), F32),
+    own_grad, ds_own = pl.pallas_call(
+        functools.partial(own_kernel, wide_dims, [place_of(kept - 1)]),
+        out_shape=[
+            jax.ShapeDtypeStruct((tokens, wide), F32),
+            jax.ShapeDtypeStruct((tokens, rows), BF16),
+        ],
+        scratch_shapes=[pltpu.VMEM((tokens, rows), BF16)],
         cost_estimate=pl.CostEstimate(
             flops=2 * rows * tokens * (wide + width),
             bytes_accessed=2 * rows * wide,
@@ -448,11 +476,14 @@
         ),
         compiler_params=params,
         name="own_gradients",
-    )(ds, weights, *queries, *handed)
+    )(row_values, *queries, *exponents[:2], *handed)
+    ds_pieces = ds_pieces + [ds_own, ds_sent]
 
     query_cotangent, rotary_cotangent = pl.pallas_call(
-        functools.partial(query_kernel, (pairs, tokens, width, rope)),
-        in_specs=[vmem] * 2,
+        functools.partial(
+            query_kernel, (pairs, tokens, width, rope), sources, len(ds_pieces)
+        ),
+        in_specs=[vmem] * (len(ds_pieces) + len(key_arrays)),
         out_specs=[hbm] * 2,
         out_shape=[
             jax.ShapeDtypeStruct(query_latent.shape, BF16),
@@ -461,6 +492,8 @@
         scratch_shapes=[
             pltpu.VMEM(query_latent.shape, BF16),
             pltpu.VMEM(query_rotary.shape, BF16),
+            pltpu.VMEM((depth, rows), BF16),
+            pltpu.VMEM((depth, wide), BF16),
             pltpu.SemaphoreType.DMA((pairs + 1,)),
         ],
         cost_estimate=pl.CostEstimate(
@@ -470,7 +503,7 @@
         ),
         compiler_params=params,
         name="query_cotangents",
-    )(ds, keys)
+    )(*ds_pieces, *key_arrays)
 
     parts = pl.pallas_call(
         functools.partial(total_kernel, len(back)),

time: 45.2 us -> 44.7 us (0.989)
    pallas_call x1, Pallas kernels: 2.63 us -> 2.18 us  [per_device(): pl.pallas_call(functools.partial(scores_kernel, (nd, kept, pairs, tokens,...]
where the time goes in v3:
time: 44.7 us; the launch traced here: 44.5 us
  starting transfers between devices  18.4 us (41%)
  waiting for transfers between devices  12 us (27%)
  Pallas kernels  10.2 us (23%)
  local copies, waits for them, and re-layouts  2.24 us (5%)
  other arithmetic  0.9 us (2%)
  between operations  0.78 us (2%)
    ppermute x13, starting transfers between devices, rotated(): lax.ppermute(value, axis, [(s, (s + steps) % count) for s in range(count)])  17.7 us
    ppermute x13, waiting for transfers between devices, rotated(): lax.ppermute(value, axis, [(s, (s + steps) % count) for s in range(count)])  11.6 us
    pallas_call x2, Pallas kernels, early_scores(): pl.pallas_call(functools.partial(early_kernel, (pairs, tokens, shard, wid...  3.15 us
    unnamed x11, local copies, waits for them, and re-layouts  2.23 us
    pallas_call x1, Pallas kernels, per_device(): pl.pallas_call(functools.partial(scores_kernel, (nd, kept, pairs, tokens,...  2.18 us
    pallas_call x1, Pallas kernels, per_device(): pl.pallas_call(functools.partial(query_kernel, (pairs, tokens, width, rop...  2.1 us
    concatenate x1, other arithmetic, per_device(): own = jnp.concatenate([latent, key_rotary, key_rotary], axis=1)  0.9 us
  transfers between devices with their start and end apart: 17, of which 11 were waited for; matrix products, arithmetic and copies ran while one was open for 0% of the time, Pallas kernels for 16%

profile of v3, /device:TPU:0, one launch (start us, length us, event | category | flops | bytes accessed | tf_op | source)
XLA Modules:
  0.0 44.5 jit_solution(9689220272997117219)
XLA Ops:
  0.6 0.9 %pad_maximum_fusion = bf16[32,640]{1,0:T(8,128)(2,1)S(1)} fusion(bf16[32,64]{1,0:T(8,128)(2,1)} %param.10, bf16[32,512]{1,0:T(8,128)(2,1)} %param.9), kind=kLoop, calls=%fused_computation | loop fusion | flops 122880 | bytes 77824 | tf_op jit(solution)/shard_map/concatenate | solution.py:328
  1.5 5.1 %collective-permute-start.2 = (bf16[32,640]{1,0:T(8,128)(2,1)S(1)}, bf16[32,640]{1,0:T(8,128)(2,1)S(1)}, u32[]{:S(2)}, u32[]{:S(2)}) collective-permute-start(bf16[32,640]{1,0:T(8,128)(2,1)S(1)} %pad_maximum_fusion), channel_id=1, source_target_pairs={{0,3},{1,0},{2,1},{3,2},{4,7},{5,4},{6,5},{7,6},{8,11},{9,8},{10,9... | collective-permute-start | bytes 122888 | tf_op jit(solution)/shard_map/ppermute | solution.py:31
  6.6 1.0 %collective-permute-start = (bf16[32,640]{1,0:T(8,128)(2,1)S(1)}, bf16[32,640]{1,0:T(8,128)(2,1)S(1)}, u32[]{:S(2)}, u32[]{:S(2)}) collective-permute-start(bf16[32,640]{1,0:T(8,128)(2,1)S(1)} %pad_maximum_fusion), channel_id=1, source_target_pairs={{0,1},{1,2},{2,3},{3,0},{4,5},{5,6},{6,7},{7,4},{8,9},{9,10},{10,1... | collective-permute-start | bytes 122888 | tf_op jit(solution)/shard_map/ppermute | solution.py:31
  7.6 0.7 %collective-permute-done.2 = bf16[32,640]{1,0:T(8,128)(2,1)S(1)} collective-permute-done((bf16[32,640]{1,0:T(8,128)(2,1)S(1)}, bf16[32,640]{1,0:T(8,128)(2,1)S(1)}, u32[]{:S(2)}, u32[]{:S(2)}) %collective-permute-start.2) | collective-permute-done | bytes 40992 | tf_op jit(solution)/shard_map/ppermute | solution.py:31
  8.3 3.2 %collective-permute-done.1 = bf16[32,640]{1,0:T(8,128)(2,1)S(1)} collective-permute-done((bf16[32,640]{1,0:T(8,128)(2,1)S(1)}, bf16[32,640]{1,0:T(8,128)(2,1)S(1)}, u32[]{:S(2)}, u32[]{:S(2)}) %collective-permute-start.1) | collective-permute-done | bytes 40992 | tf_op jit(solution)/shard_map/ppermute | solution.py:31
  11.5 0.9 %collective-permute-done = bf16[32,640]{1,0:T(8,128)(2,1)S(1)} collective-permute-done((bf16[32,640]{1,0:T(8,128)(2,1)S(1)}, bf16[32,640]{1,0:T(8,128)(2,1)S(1)}, u32[]{:S(2)}, u32[]{:S(2)}) %collective-permute-start) | collective-permute-done | bytes 40992 | tf_op jit(solution)/shard_map/ppermute | solution.py:31
  12.5 1.5 %collective-permute-start.3 = (bf16[128,640]{1,0:T(8,128)(2,1)S(1)}, bf16[128,640]{1,0:T(8,128)(2,1)S(1)}, u32[]{:S(2)}, u32[]{:S(2)}) collective-permute-start(bf16[128,640]{1,0:T(8,128)(2,1)S(1)} %constant_dynamic-update-slice_fusion.refs_1_.refs_6_.refs_3_), channel_id=1, source_target_pairs={{0,8},{4,12},{8,16},{12,20},{16,24},{20,28},{24,0},{28,4},{1,9},{5... | collective-permute-start | bytes 491528 | tf_op jit(solution)/shard_map/ppermute | solution.py:31
  14.0 1.5 %collective-permute-start.4 = (bf16[128,640]{1,0:T(8,128)(2,1)S(1)}, bf16[128,640]{1,0:T(8,128)(2,1)S(1)}, u32[]{:S(2)}, u32[]{:S(2)}) collective-permute-start(bf16[128,640]{1,0:T(8,128)(2,1)S(1)} %constant_dynamic-update-slice_fusion.refs_1_.refs_6_.refs_3_), channel_id=1, source_target_pairs={{0,16},{4,20},{8,24},{12,28},{16,0},{20,4},{24,8},{28,12},{1,17},{... | collective-permute-start | bytes 491528 | tf_op jit(solution)/shard_map/ppermute | solution.py:31
  15.5 1.2 %copy-done = bf16[128,4096]{1,0:T(8,128)(2,1)S(1)} copy-done((bf16[128,4096]{1,0:T(8,128)(2,1)S(1)}, bf16[128,4096]{1,0:T(8,128)(2,1)}, u32[]{:S(2)}) %copy-start) | copy-done | bytes 1048600
  17.0 1.0 %copy-done.1 = bf16[128,4096]{1,0:T(8,128)(2,1)S(1)} copy-done((bf16[128,4096]{1,0:T(8,128)(2,1)S(1)}, bf16[128,4096]{1,0:T(8,128)(2,1)}, u32[]{:S(2)}) %copy-start.1) | copy-done | bytes 1048600
  18.9 1.6 %shard_map.95 = (f32[256,1024]{1,0:T(8,128)S(1)}, f32[256,1024]{1,0:T(8,128)S(1)}, f32[8,1024]{1,0:T(8,128)S(1)}) custom-call(s32[1,5]{1,0:T(1,128)S(1)} %copy-done.3, bf16[1024,640]{1,0:T(8,128)(2,1)S(1)} %shard_map.93.q2_ref, bf16[1024,512]{1,0:T(8,128)(2,1)S(1)} %shard_map.94.u2_ref, bf16[128,640]{1,0:T(8,128)(2,1)S(1)} %collective-permute-done.3.refs_0_.refs_7_.refs_4_, ...), custom_call_target="tpu_custom_call" | custom-call | flops 603979776 | bytes 2097152 | tf_op jit(solution)/shard_map/pallas_call | solution.py:354
  20.5 1.0 %collective-permute-done.4.refs_0_.refs_8_.refs_5_ = bf16[128,640]{1,0:T(8,128)(2,1)S(1)} collective-permute-done((bf16[128,640]{1,0:T(8,128)(2,1)S(1)}, bf16[128,640]{1,0:T(8,128)(2,1)S(1)}, u32[]{:S(2)}, u32[]{:S(2)}) %collective-permute-start.4) | collective-permute-done | bytes 163872 | tf_op jit(solution)/shard_map/ppermute | solution.py:31
  21.5 1.5 %shard_map.96 = (f32[256,1024]{1,0:T(8,128)S(1)}, f32[256,1024]{1,0:T(8,128)S(1)}, f32[8,1024]{1,0:T(8,128)S(1)}) custom-call(s32[1,5]{1,0:T(1,128)S(1)} %copy-done.3, bf16[1024,640]{1,0:T(8,128)(2,1)S(1)} %shard_map.93.q2_ref, bf16[1024,512]{1,0:T(8,128)(2,1)S(1)} %shard_map.94.u2_ref, bf16[128,640]{1,0:T(8,128)(2,1)S(1)} %collective-permute-done.4.refs_0_.refs_8_.refs_5_, ...), custom_call_target="tpu_custom_call" | custom-call | flops 603979776 | bytes 2097152 | tf_op jit(solution)/shard_map/pallas_call | solution.py:354
  23.0 2.2 %scores.1 = (bf16[256,1024]{1,0:T(8,128)(2,1)S(1)}, f32[8,1024]{1,0:T(8,128)S(1)}, bf16[256,640]{1,0:T(8,128)(2,1)S(1)}) custom-call(s32[1,5]{1,0:T(1,128)S(1)} %copy-done.3, bf16[1024,640]{1,0:T(8,128)(2,1)S(1)} %shard_map.93.q2_ref, bf16[1024,512]{1,0:T(8,128)(2,1)S(1)} %shard_map.94.u2_ref, f32[256,1024]{1,0:T(8,128)S(1)} %get-tuple-element.51.refs_0_.e_ref, ...), custom_call_target="tpu_custom_call" | custom-call | flops 905969664 | bytes 5242880 | tf_op jit(solution)/shard_map/scores/pallas_call | solution.py:389
  25.8 0.9 %late_gradients.1 = (f32[256,640]{1,0:T(8,128)S(1)}, bf16[256,1024]{1,0:T(8,128)(2,1)S(1)}) custom-call(f32[8,1024]{1,0:T(8,128)S(1)} %get-tuple-element.58.rows_ref, bf16[1024,640]{1,0:T(8,128)(2,1)S(1)} %shard_map.93.q2_ref, bf16[1024,512]{1,0:T(8,128)(2,1)S(1)} %shard_map.94.u2_ref, f32[256,1024]{1,0:T(8,128)S(1)} %get-tuple-element.51.refs_0_.e_ref, ...), custom_call_target="tpu_custom_call" | custom-call | flops 603979776 | bytes 2621440 | tf_op jit(solution)/shard_map/late_gradients/pallas_call | solution.py:424
  27.2 1.0 %collective-permute-start.9 = (bf16[128,640]{1,0:T(8,128)(2,1)S(1)}, bf16[128,640]{1,0:T(8,128)(2,1)S(1)}, u32[]{:S(2)}, u32[]{:S(2)}) collective-permute-start(bf16[128,640]{1,0:T(8,128)(2,1)S(1)} %get-tuple-element.67), channel_id=1, source_target_pairs={{0,24},{4,28},{8,0},{12,4},{16,8},{20,12},{24,16},{28,20},{1,25},{... | collective-permute-start | bytes 491528 | tf_op jit(solution)/shard_map/ppermute | solution.py:31
  29.3 2.0 %collective-permute-start.15 = (bf16[32,640]{1,0:T(8,128)(2,1)S(1)}, bf16[32,640]{1,0:T(8,128)(2,1)S(1)}, u32[]{:S(2)}, u32[]{:S(2)}) collective-permute-start(bf16[32,640]{1,0:T(8,128)(2,1)S(1)} %get-tuple-element.75), channel_id=1, source_target_pairs={{0,1},{1,2},{2,3},{3,0},{4,5},{5,6},{6,7},{7,4},{8,9},{9,10},{10,1... | collective-permute-start | bytes 122888 | tf_op jit(solution)/shard_map/ppermute | solution.py:31
  31.8 0.7 %collective-permute-done.13.refs_0_ = bf16[32,640]{1,0:T(8,128)(2,1)S(1)} collective-permute-done((bf16[32,640]{1,0:T(8,128)(2,1)S(1)}, bf16[32,640]{1,0:T(8,128)(2,1)S(1)}, u32[]{:S(2)}, u32[]{:S(2)}) %collective-permute-start.13) | collective-permute-done | bytes 40992 | tf_op jit(solution)/shard_map/ppermute | solution.py:31
  32.6 2.0 %collective-permute-done.14.refs_1_ = bf16[32,640]{1,0:T(8,128)(2,1)S(1)} collective-permute-done((bf16[32,640]{1,0:T(8,128)(2,1)S(1)}, bf16[32,640]{1,0:T(8,128)(2,1)S(1)}, u32[]{:S(2)}, u32[]{:S(2)}) %collective-permute-start.14) | collective-permute-done | bytes 40992 | tf_op jit(solution)/shard_map/ppermute | solution.py:31
  35.1 1.2 %collective-permute-start.16 = (bf16[32,640]{1,0:T(8,128)(2,1)S(1)}, bf16[32,640]{1,0:T(8,128)(2,1)S(1)}, u32[]{:S(2)}, u32[]{:S(2)}) collective-permute-start(bf16[32,640]{1,0:T(8,128)(2,1)S(1)} %sum_four.1), channel_id=1, source_target_pairs={{0,16},{4,20},{8,24},{12,28},{16,0},{20,4},{24,8},{28,12},{1,17},{... | collective-permute-start | bytes 122888 | tf_op jit(solution)/shard_map/ppermute | solution.py:31
  36.4 1.6 %collective-permute-start.10 = (bf16[32,640]{1,0:T(8,128)(2,1)S(1)}, bf16[32,640]{1,0:T(8,128)(2,1)S(1)}, u32[]{:S(2)}, u32[]{:S(2)}) collective-permute-start(bf16[32,640]{1,0:T(8,128)(2,1)S(1)} %get-tuple-element.69), channel_id=1, source_target_pairs={{0,3},{1,0},{2,1},{3,2},{4,7},{5,4},{6,5},{7,6},{8,11},{9,8},{10,9... | collective-permute-start | bytes 122888 | tf_op jit(solution)/shard_map/ppermute | solution.py:31
  38.0 1.5 %collective-permute-start.12 = (bf16[32,640]{1,0:T(8,128)(2,1)S(1)}, bf16[32,640]{1,0:T(8,128)(2,1)S(1)}, u32[]{:S(2)}, u32[]{:S(2)}) collective-permute-start(bf16[32,640]{1,0:T(8,128)(2,1)S(1)} %get-tuple-element.71), channel_id=1, source_target_pairs={{0,1},{1,2},{2,3},{3,0},{4,5},{5,6},{6,7},{7,4},{8,9},{9,10},{10,1... | collective-permute-start | bytes 122888 | tf_op jit(solution)/shard_map/ppermute | solution.py:31
  39.6 2.1 %query_cotangents.1 = (bf16[128,4096]{1,0:T(8,128)(2,1)}, bf16[128,512]{1,0:T(8,128)(2,1)}) custom-call(bf16[256,1024]{1,0:T(8,128)(2,1)S(1)} %get-tuple-element.59.refs_0_, bf16[128,1024]{1,0:T(8,128)(2,1)S(1)} %get-tuple-element.61.refs_1_, bf16[256,1024]{1,0:T(8,128)(2,1)S(1)} %get-tuple-element.62.refs_2_, ...), custom_call_target="tpu_custom_call" | custom-call | flops 838860800 | bytes 2621440 | tf_op jit(solution)/shard_map/query_cotangents/pallas_call | solution.py:482
  41.7 1.5 %collective-permute-done.11.refs_1_ = bf16[32,640]{1,0:T(8,128)(2,1)S(1)} collective-permute-done((bf16[32,640]{1,0:T(8,128)(2,1)S(1)}, bf16[32,640]{1,0:T(8,128)(2,1)S(1)}, u32[]{:S(2)}, u32[]{:S(2)}) %collective-permute-start.11) | collective-permute-done | bytes 40992 | tf_op jit(solution)/shard_map/ppermute | solution.py:31
  (35 shorter events, 5.8 us)
Async XLA Ops:
  0.6 16.4 %copy-start.2 = (bf16[128,512]{1,0:T(8,128)(2,1)S(1)}, bf16[128,512]{1,0:T(8,128)(2,1)}, u32[]{:S(2)}) copy-start(bf16[128,512]{1,0:T(8,128)(2,1)} %refs_0_.1) | copy-start | bytes 393220
  1.5 6.8 %collective-permute-start.2 = (bf16[32,640]{1,0:T(8,128)(2,1)S(1)}, bf16[32,640]{1,0:T(8,128)(2,1)S(1)}, u32[]{:S(2)}, u32[]{:S(2)}) collective-permute-start(bf16[32,640]{1,0:T(8,128)(2,1)S(1)} %pad_maximum_fusion), channel_id=1, source_target_pairs={{0,3},{1,0},{2,1},{3,2},{4,7},{5,4},{6,5},{7,6},{8,11},{9,8},{10,9... | collective-permute-start | bytes 122888 | tf_op jit(solution)/shard_map/ppermute | solution.py:31
  6.6 4.9 %collective-permute-start.1 = (bf16[32,640]{1,0:T(8,128)(2,1)S(1)}, bf16[32,640]{1,0:T(8,128)(2,1)S(1)}, u32[]{:S(2)}, u32[]{:S(2)}) collective-permute-start(bf16[32,640]{1,0:T(8,128)(2,1)S(1)} %pad_maximum_fusion), channel_id=1, source_target_pairs={{0,2},{1,3},{2,0},{3,1},{4,6},{5,7},{6,4},{7,5},{8,10},{9,11},{10,... | collective-permute-start | bytes 122888 | tf_op jit(solution)/shard_map/ppermute | solution.py:31
  6.6 5.8 %collective-permute-start = (bf16[32,640]{1,0:T(8,128)(2,1)S(1)}, bf16[32,640]{1,0:T(8,128)(2,1)S(1)}, u32[]{:S(2)}, u32[]{:S(2)}) collective-permute-start(bf16[32,640]{1,0:T(8,128)(2,1)S(1)} %pad_maximum_fusion), channel_id=1, source_target_pairs={{0,1},{1,2},{2,3},{3,0},{4,5},{5,6},{6,7},{7,4},{8,9},{9,10},{10,1... | collective-permute-start | bytes 122888 | tf_op jit(solution)/shard_map/ppermute | solution.py:31
  12.5 6.4 %collective-permute-start.3 = (bf16[128,640]{1,0:T(8,128)(2,1)S(1)}, bf16[128,640]{1,0:T(8,128)(2,1)S(1)}, u32[]{:S(2)}, u32[]{:S(2)}) collective-permute-start(bf16[128,640]{1,0:T(8,128)(2,1)S(1)} %constant_dynamic-update-slice_fusion.refs_1_.refs_6_.refs_3_), channel_id=1, source_target_pairs={{0,8},{4,12},{8,16},{12,20},{16,24},{20,28},{24,0},{28,4},{1,9},{5... | collective-permute-start | bytes 491528 | tf_op jit(solution)/shard_map/ppermute | solution.py:31
  14.0 7.4 %collective-permute-start.4 = (bf16[128,640]{1,0:T(8,128)(2,1)S(1)}, bf16[128,640]{1,0:T(8,128)(2,1)S(1)}, u32[]{:S(2)}, u32[]{:S(2)}) collective-permute-start(bf16[128,640]{1,0:T(8,128)(2,1)S(1)} %constant_dynamic-update-slice_fusion.refs_1_.refs_6_.refs_3_), channel_id=1, source_target_pairs={{0,16},{4,20},{8,24},{12,28},{16,0},{20,4},{24,8},{28,12},{1,17},{... | collective-permute-start | bytes 491528 | tf_op jit(solution)/shard_map/ppermute | solution.py:31
  15.5 1.2 %copy-start = (bf16[128,4096]{1,0:T(8,128)(2,1)S(1)}, bf16[128,4096]{1,0:T(8,128)(2,1)}, u32[]{:S(2)}) copy-start(bf16[128,4096]{1,0:T(8,128)(2,1)} %x_ref.3) | copy-start | bytes 3145732
  16.8 1.2 %copy-start.1 = (bf16[128,4096]{1,0:T(8,128)(2,1)S(1)}, bf16[128,4096]{1,0:T(8,128)(2,1)}, u32[]{:S(2)}) copy-start(bf16[128,4096]{1,0:T(8,128)(2,1)} %x_ref.2) | copy-start | bytes 3145732
  18.0 0.9 %copy-start.3 = (s32[1,5]{1,0:T(1,128)S(1)}, s32[1,5]{1,0:T(1,128)}, u32[]{:S(2)}) copy-start(s32[1,5]{1,0:T(1,128)} %pattern_ref.5) | copy-start | bytes 64
  18.3 3.2 %collective-permute-start.5 = (bf16[128,640]{1,0:T(8,128)(2,1)S(1)}, bf16[128,640]{1,0:T(8,128)(2,1)S(1)}, u32[]{:S(2)}, u32[]{:S(2)}) collective-permute-start(bf16[128,640]{1,0:T(8,128)(2,1)S(1)} %constant_dynamic-update-slice_fusion.refs_1_.refs_6_.refs_3_), channel_id=1, source_target_pairs={{0,4},{4,0},{8,12},{12,8},{16,20},{20,16},{24,28},{28,24},{1,5},{5... | collective-permute-start | bytes 491528 | tf_op jit(solution)/shard_map/ppermute | solution.py:36
  18.8 2.6 %collective-permute-start.6 = (bf16[128,640]{1,0:T(8,128)(2,1)S(1)}, bf16[128,640]{1,0:T(8,128)(2,1)S(1)}, u32[]{:S(2)}, u32[]{:S(2)}) collective-permute-start(bf16[128,640]{1,0:T(8,128)(2,1)S(1)} %collective-permute-done.3.refs_0_.refs_7_.refs_4_), channel_id=1, source_target_pairs={{0,4},{4,0},{8,12},{12,8},{16,20},{20,16},{24,28},{28,24},{1,5},{5... | collective-permute-start | bytes 491528 | tf_op jit(solution)/shard_map/ppermute | solution.py:36
  21.4 1.6 %collective-permute-start.7 = (bf16[128,640]{1,0:T(8,128)(2,1)S(1)}, bf16[128,640]{1,0:T(8,128)(2,1)S(1)}, u32[]{:S(2)}, u32[]{:S(2)}) collective-permute-start(bf16[128,640]{1,0:T(8,128)(2,1)S(1)} %collective-permute-done.4.refs_0_.refs_8_.refs_5_), channel_id=1, source_target_pairs={{0,4},{4,0},{8,12},{12,8},{16,20},{20,16},{24,28},{28,24},{1,5},{5... | collective-permute-start | bytes 491528 | tf_op jit(solution)/shard_map/ppermute | solution.py:36
  25.2 1.8 %collective-permute-start.8 = (bf16[256,640]{1,0:T(8,128)(2,1)S(1)}, bf16[256,640]{1,0:T(8,128)(2,1)S(1)}, u32[]{:S(2)}, u32[]{:S(2)}) collective-permute-start(bf16[256,640]{1,0:T(8,128)(2,1)S(1)} %get-tuple-element.60), channel_id=1, source_target_pairs={{0,4},{4,0},{8,12},{12,8},{16,20},{20,16},{24,28},{28,24},{1,5},{5... | collective-permute-start | bytes 983048 | tf_op jit(solution)/shard_map/ppermute | solution.py:36
  27.2 9.2 %collective-permute-start.9 = (bf16[128,640]{1,0:T(8,128)(2,1)S(1)}, bf16[128,640]{1,0:T(8,128)(2,1)S(1)}, u32[]{:S(2)}, u32[]{:S(2)}) collective-permute-start(bf16[128,640]{1,0:T(8,128)(2,1)S(1)} %get-tuple-element.67), channel_id=1, source_target_pairs={{0,24},{4,28},{8,0},{12,4},{16,8},{20,12},{24,16},{28,20},{1,25},{... | collective-permute-start | bytes 491528 | tf_op jit(solution)/shard_map/ppermute | solution.py:31
  28.1 4.4 %collective-permute-start.13 = (bf16[32,640]{1,0:T(8,128)(2,1)S(1)}, bf16[32,640]{1,0:T(8,128)(2,1)S(1)}, u32[]{:S(2)}, u32[]{:S(2)}) collective-permute-start(bf16[32,640]{1,0:T(8,128)(2,1)S(1)} %get-tuple-element.73), channel_id=1, source_target_pairs={{0,3},{1,0},{2,1},{3,2},{4,7},{5,4},{6,5},{7,6},{8,11},{9,8},{10,9... | collective-permute-start | bytes 122888 | tf_op jit(solution)/shard_map/ppermute | solution.py:31
  28.8 5.8 %collective-permute-start.14 = (bf16[32,640]{1,0:T(8,128)(2,1)S(1)}, bf16[32,640]{1,0:T(8,128)(2,1)S(1)}, u32[]{:S(2)}, u32[]{:S(2)}) collective-permute-start(bf16[32,640]{1,0:T(8,128)(2,1)S(1)} %get-tuple-element.74), channel_id=1, source_target_pairs={{0,2},{1,3},{2,0},{3,1},{4,6},{5,7},{6,4},{7,5},{8,10},{9,11},{10,... | collective-permute-start | bytes 122888 | tf_op jit(solution)/shard_map/ppermute | solution.py:31
  29.3 5.8 %collective-permute-start.15 = (bf16[32,640]{1,0:T(8,128)(2,1)S(1)}, bf16[32,640]{1,0:T(8,128)(2,1)S(1)}, u32[]{:S(2)}, u32[]{:S(2)}) collective-permute-start(bf16[32,640]{1,0:T(8,128)(2,1)S(1)} %get-tuple-element.75), channel_id=1, source_target_pairs={{0,1},{1,2},{2,3},{3,0},{4,5},{5,6},{6,7},{7,4},{8,9},{9,10},{10,1... | collective-permute-start | bytes 122888 | tf_op jit(solution)/shard_map/ppermute | solution.py:31
  35.1 6.6 %collective-permute-start.16 = (bf16[32,640]{1,0:T(8,128)(2,1)S(1)}, bf16[32,640]{1,0:T(8,128)(2,1)S(1)}, u32[]{:S(2)}, u32[]{:S(2)}) collective-permute-start(bf16[32,640]{1,0:T(8,128)(2,1)S(1)} %sum_four.1), channel_id=1, source_target_pairs={{0,16},{4,20},{8,24},{12,28},{16,0},{20,4},{24,8},{28,12},{1,17},{... | collective-permute-start | bytes 122888 | tf_op jit(solution)/shard_map/ppermute | solution.py:31
  36.4 5.3 %collective-permute-start.10 = (bf16[32,640]{1,0:T(8,128)(2,1)S(1)}, bf16[32,640]{1,0:T(8,128)(2,1)S(1)}, u32[]{:S(2)}, u32[]{:S(2)}) collective-permute-start(bf16[32,640]{1,0:T(8,128)(2,1)S(1)} %get-tuple-element.69), channel_id=1, source_target_pairs={{0,3},{1,0},{2,1},{3,2},{4,7},{5,4},{6,5},{7,6},{8,11},{9,8},{10,9... | collective-permute-start | bytes 122888 | tf_op jit(solution)/shard_map/ppermute | solution.py:31
  38.0 5.2 %collective-permute-start.11 = (bf16[32,640]{1,0:T(8,128)(2,1)S(1)}, bf16[32,640]{1,0:T(8,128)(2,1)S(1)}, u32[]{:S(2)}, u32[]{:S(2)}) collective-permute-start(bf16[32,640]{1,0:T(8,128)(2,1)S(1)} %get-tuple-element.70), channel_id=1, source_target_pairs={{0,2},{1,3},{2,0},{3,1},{4,6},{5,7},{6,4},{7,5},{8,10},{9,11},{10,... | collective-permute-start | bytes 122888 | tf_op jit(solution)/shard_map/ppermute | solution.py:31
  38.0 5.8 %collective-permute-start.12 = (bf16[32,640]{1,0:T(8,128)(2,1)S(1)}, bf16[32,640]{1,0:T(8,128)(2,1)S(1)}, u32[]{:S(2)}, u32[]{:S(2)}) collective-permute-start(bf16[32,640]{1,0:T(8,128)(2,1)S(1)} %get-tuple-element.71), channel_id=1, source_target_pairs={{0,1},{1,2},{2,3},{3,0},{4,5},{5,6},{6,7},{7,4},{8,9},{9,10},{10,1... | collective-permute-start | bytes 122888 | tf_op jit(solution)/shard_map/ppermute | solution.py:31
